TPU v7x, 128 devices: a whole 4x4x4 slice. The times are simulated.
128 devices in a mesh: replica: 2 (over core), fsdp: 16 (over y, x), tensor: 4 (over z).
Axes of the slice: x: 4, y: 4, z: 4, core: 2. Of those that a mesh axis runs over, the one named last changes fastest.
Arguments:
- grads: bfloat16 [2, 2, 4096, 14336], P('replica', None, 'fsdp', 'tensor'), may hold values from -6 to 6
- momentum: bfloat16 [2, 4096, 14336], P(None, 'fsdp', 'tensor'), may hold values from -50 to 50, as said below
- basis: bfloat16 [2, 14336, 512], P(None, 'tensor'), may hold values from -0.046875 to 0.046875
Outputs:
- momentum_new: bfloat16 [2, 4096, 14336], P(None, 'fsdp', 'tensor')
- update: bfloat16 [2, 4096, 14336], P(None, 'fsdp', 'tensor')
- basis_new: bfloat16 [2, 14336, 512], P(None, 'tensor')
Inputs may be any that keep to these rules, and one draw needn't show every extreme that they name: `momentum`: entries are finite.
All inputs are finite; a program needn't handle non-finite values.
Results may differ from a plain program's by a relative error of at most 0.028.
Values may be sent and summed in bfloat16 or wider, within the bound.
A program may use at most 128 MiB of HBM per device.

v0:
```python
import functools
import math

import jax
import jax.numpy as jnp
from jax import lax
from jax.sharding import Mesh
from jax.sharding import PartitionSpec as P

FEATURES = 4096
UNITS = 14336
RANK = 512
FSDP = ("fsdp_0", "fsdp_1")
REPLICA_FSDP_TENSOR = ("replica", "fsdp_0", "fsdp_1", "tensor")
REPLICA_FSDP = ("replica", "fsdp_0", "fsdp_1")


momentum_decay = 0.95


def from_everyone(x, axis):
    size = lax.axis_size(axis)
    return lax.all_to_all(jnp.broadcast_to(x[None], (size, *x.shape)), axis, 0, 0, tiled=True)


def of_everyone(x, axis):
    everything = from_everyone(x, axis)
    return jnp.sum(everything.astype(jnp.float32), axis=0)


def in_blocks(x, dim, size):
    before, after = (x.shape[:dim], x.shape[dim + 1 :])
    return jnp.moveaxis(x.reshape(*before, size, -1, *after), dim, 0)


def piece_ends(length, count):
    unit = 8 if length >= 8 * count else 1
    return [length // unit * k // count * unit for k in range(1, count)]


def own_block(pieces, axes, turns):
    dims = [lax.axis_size(a) for a in axes]
    pieces = pieces.reshape(*dims, *pieces.shape[1:])
    pieces = pieces.transpose(*turns, *range(len(axes), pieces.ndim))
    pieces = pieces.reshape(-1, *pieces.shape[len(axes) :])
    for k in turns:
        pieces = lax.psum_scatter(pieces, axes[k], scatter_dimension=0, tiled=True)
    return pieces[0]


def spread_scatter(x, axes, dim):
    pieces = in_blocks(x, dim, lax.axis_size(axes))
    cut = max(range(1, max(2, pieces.ndim - 1)), key=lambda d: pieces.shape[d])
    count, done = (len(axes), [])
    for initial, section in enumerate(
        jnp.split(pieces, piece_ends(pieces.shape[cut], count), axis=cut)
    ):
        if section.size:
            turns = [(initial + k) % count for k in range(count)]
            done.append(own_block(section, axes, turns))
    return jnp.concatenate(done, axis=cut - 1)


def over_axes(x, axes):
    return functools.reduce(lax.psum, axes, x)


def total_of_pieces(x, axis):
    return lax.all_gather(x, axis).astype(jnp.float32).sum(0)


def orthonormal(projected, factor):

    def solve_one(lower_mat, rows_mat):
        return jax.scipy.linalg.solve_triangular(lower_mat, rows_mat.T, lower=True).T

    return jax.vmap(solve_one)(factor, projected).astype(jnp.bfloat16)


def power_step(total_grad, moment, right):
    blended = (moment.astype(jnp.float32) + total_grad).astype(jnp.bfloat16)
    partial_value = jnp.einsum("wmc,wcr->wmr", blended, right, preferred_element_type=jnp.float32)
    projected = of_everyone(partial_value.astype(jnp.bfloat16), "tensor").astype(jnp.float32)
    gram_local = jnp.einsum(
        "wmr,wms->wrs", projected, projected, preferred_element_type=jnp.float32
    )
    gram_matrix = lax.psum(gram_local.astype(jnp.bfloat16), FSDP).astype(jnp.float32)
    factor = jnp.linalg.cholesky(gram_matrix)
    left_basis = orthonormal(projected, factor)
    half = blended.shape[2] // lax.axis_size("replica")
    offset = lax.axis_index("replica") * half
    kept_half = half // lax.axis_size(FSDP)
    columns = lax.dynamic_slice_in_dim(blended, offset, kept_half * lax.axis_size(FSDP), 2)
    back_piece = spread_scatter(
        jnp.einsum("wmc,wmr->cwr", columns, left_basis, preferred_element_type=jnp.float32).astype(
            jnp.bfloat16
        ),
        FSDP,
        0,
    ).astype(jnp.float32)
    squares = over_axes(jnp.sum(back_piece * back_piece, axis=0), REPLICA_FSDP_TENSOR)
    back_b = back_piece.astype(jnp.bfloat16)
    right_rows = lax.all_gather(back_b, REPLICA_FSDP, axis=0, tiled=True)
    inverse = 1.0 / (jnp.sqrt(squares) + 1e-06)
    normed = (right_rows.astype(jnp.float32) * inverse[None, :, :]).astype(jnp.bfloat16)
    feedback = jnp.einsum(
        "wmr,cwr->wmc", left_basis, right_rows, preferred_element_type=jnp.float32
    )
    momentum_new = (blended.astype(jnp.float32) - (1.0 - momentum_decay) * feedback).astype(
        jnp.bfloat16
    )
    scale = math.sqrt(FEATURES * UNITS / RANK)
    update = (
        scale * jnp.einsum("wmr,cwr->wmc", left_basis, normed, preferred_element_type=jnp.float32)
    ).astype(jnp.bfloat16)
    basis_new = jnp.transpose(normed, (1, 0, 2))
    return (momentum_new, update, basis_new)


def summed_grads(grads):
    return total_of_pieces(grads[0].astype(jnp.float32).astype(jnp.bfloat16), "replica").astype(
        jnp.float32
    )


def shards(grads, momentum, basis):
    return power_step(summed_grads(grads), momentum, basis)


def solution(mesh):
    torus = Mesh(
        mesh.devices.reshape(mesh.shape["replica"], 4, 4, mesh.shape["tensor"]),
        ("replica", "fsdp_0", "fsdp_1", "tensor"),
    )
    return jax.shard_map(
        shards,
        mesh=torus,
        in_specs=(
            P("replica", None, FSDP, "tensor"),
            P(None, FSDP, "tensor"),
            P(None, "tensor", None),
        ),
        out_specs=(P(None, FSDP, "tensor"), P(None, FSDP, "tensor"), P(None, "tensor", None)),
        check_vma=False,
    )
```

profile of v0, /device:TPU:1, one launch (start us, length us, event | category | flops | bytes accessed | tf_op | source)
XLA Modules:
  0.0 627.2 jit_solution(4297394936807727248)
XLA Ops:
  7.9 26.3 %all-gather.3.cloned.1.call-done = bf16[2,2,256,3584]{3,2,1,0:T(8,128)(2,1)} async-done(((bf16[1,2,256,3584]{3,2,1,0:T(8,128)(2,1)}), bf16[2,2,256,3584]{3,2,1,0:T(8,128)(2,1)}) %all-gather.3.cloned.1.call-update) | async-done | bytes 7340048 | tf_op jit(solution)/shard_map/all_gather | solution.py:69
  34.3 5.3 convert_reduce_fusion
  40.7 6.5 %convolution_convert_fusion.2 = bf16[2,256,512]{2,1,0:T(8,128)(2,1)S(1)} fusion(bf16[2,256,3584]{2,1,0:T(8,128)(2,1)S(1)} %add_convert_fusion, bf16[2,3584,512]{2,1,0:T(8,128)(2,1)} %param.5), kind=kOutput, calls=%fused_computation.16 | convolution fusion | flops 1879310336 | bytes 11534336 | tf_op jit(solution)/shard_map/wmc,wcr->wmr/dot_general | solution.py:82
  47.4 30.0 %all_to_all.5 = bf16[4,2,256,512]{3,2,1,0:T(8,128)(2,1)S(1)} all-to-all(bf16[4,2,256,512]{3,2,1,0:T(8,128)(2,1)S(1)} %broadcast_in_dim.4), channel_id=1, replica_groups=mesh['replica'=2,'fsdp_0'=4,'fsdp_1'=4,'tensor'=4] {'tensor'}, dimensions={0} | all-to-all | bytes 4194304 | tf_op jit(solution)/shard_map/all_to_all | solution.py:23
  80.8 84.1 %all-reduce.3.cloned.1.call-done = bf16[2,512,512]{1,2,0:T(8,128)(2,1)} async-done(((bf16[2,512,512]{1,2,0:T(8,128)(2,1)}), bf16[2,512,512]{1,2,0:T(8,128)(2,1)}) %all-reduce.3.cloned.1.call-update) | async-done | bytes 1048592 | tf_op jit(solution)/shard_map/psum | solution.py:87
  168.2 23.5 %custom-call.35 = f32[2,128,128]{2,1,0:T(8,128)S(1)} custom-call(f32[2,128,128]{2,1,0:T(8,128)S(1)} %cholesky.274), custom_call_target="Cholesky" | custom-call | tf_op jit(solution)/shard_map/jit(cholesky)/cholesky | solution.py:88
  191.7 19.7 %custom-call.36 = f32[2,1,128,128]{2,3,1,0:T(8,128)S(1)} custom-call(f32[2,1,128,128]{3,2,1,0:T(8,128)S(1)} %select_bitcast_fusion.2), custom_call_target="InvertDiagBlocksLowerTriangular" | custom-call | tf_op jit(solution)/shard_map/jit(cholesky)/cholesky | solution.py:88
  214.7 23.5 %custom-call.37 = f32[2,128,128]{2,1,0:T(8,128)S(1)} custom-call(f32[2,128,128]{2,1,0:T(8,128)S(1)} %cholesky.278), custom_call_target="Cholesky" | custom-call | tf_op jit(solution)/shard_map/jit(cholesky)/cholesky | solution.py:88
  238.1 19.9 %custom-call.38 = f32[2,1,128,128]{2,3,1,0:T(8,128)S(1)} custom-call(f32[2,1,128,128]{3,2,1,0:T(8,128)S(1)} %get-tuple-element.30), custom_call_target="InvertDiagBlocksLowerTriangular" | custom-call | tf_op jit(solution)/shard_map/jit(cholesky)/cholesky | solution.py:88
  260.0 23.5 %custom-call.39 = f32[2,128,128]{2,1,0:T(8,128)S(1)} custom-call(f32[2,128,128]{2,1,0:T(8,128)S(1)} %cholesky.283), custom_call_target="Cholesky" | custom-call | tf_op jit(solution)/shard_map/jit(cholesky)/cholesky | solution.py:88
  283.5 19.7 %custom-call.40 = f32[2,1,128,128]{2,3,1,0:T(8,128)S(1)} custom-call(f32[2,1,128,128]{3,2,1,0:T(8,128)S(1)} %get-tuple-element.28), custom_call_target="InvertDiagBlocksLowerTriangular" | custom-call | tf_op jit(solution)/shard_map/jit(cholesky)/cholesky | solution.py:88
  305.0 23.9 %custom-call.41 = f32[2,128,128]{2,1,0:T(8,128)S(1)} custom-call(f32[2,128,128]{2,1,0:T(8,128)S(1)} %convolution_subtract_fusion.5), custom_call_target="Cholesky" | custom-call | tf_op jit(solution)/shard_map/jit(cholesky)/cholesky | solution.py:88
  331.0 14.5 %while.1 = (s32[]{:T(128)}, f32[2,512,512]{2,1,0:T(8,128)}, s32[4,2]{0,1:T(2,128)S(1)}, f32[4,2,128,128]{3,2,0,1:T(8,128)}, s32[]{:T(128)}) while((s32[]{:T(128)}, f32[2,512,512]{2,1,0:T(8,128)}, s32[4,2]{0,1:T(2,128)S(1)}, f32[4,2,128,128]{3,2,0,1:T(8,128)}, s32[]{:T(128)}) %tuple.36), condition=%wide.while_cond, body=%wide.while_body.sunk | while | flops 2 | bytes 263277 | solution.py:75
  345.5 79.4 %custom-call.42 = f32[2,4,128,128]{2,3,1,0:T(8,128)S(1)} custom-call(f32[2,4,128,128]{3,2,1,0:T(8,128)} %bitcast.91), custom_call_target="InvertDiagBlocksLowerTriangular" | custom-call | tf_op jit(solution)/shard_map/vmap(jit(_solve_triangular))/triangular_solve | solution.py:75
  434.2 5.9 copy.77
  445.6 26.8 %reduce-scatter.9.cloned.1.call-done = bf16[4,56,2,512]{3,1,2,0:T(8,128)(2,1)} async-done(((bf16[16,56,2,512]{3,1,2,0:T(8,128)(2,1)}), bf16[4,56,2,512]{3,1,2,0:T(8,128)(2,1)}) %reduce-scatter.9.cloned.1.call-update) | async-done | bytes 458768 | tf_op jit(solution)/shard_map/reduce_scatter | solution.py:47
  472.5 30.1 %reduce-scatter.5.cloned.1.call-done = bf16[4,56,2,512]{3,1,2,0:T(8,128)(2,1)} async-done(((bf16[16,56,2,512]{3,1,2,0:T(8,128)(2,1)}), bf16[4,56,2,512]{3,1,2,0:T(8,128)(2,1)}) %reduce-scatter.5.cloned.1.call-update) | async-done | bytes 458768 | tf_op jit(solution)/shard_map/reduce_scatter | solution.py:47
  502.7 21.0 %reduce-scatter.11.cloned.1.call-done = bf16[1,56,2,512]{3,1,2,0:T(8,128)(2,1)} async-done(((bf16[4,56,2,512]{3,1,2,0:T(8,128)(2,1)}), bf16[1,56,2,512]{3,1,2,0:T(8,128)(2,1)}) %reduce-scatter.11.cloned.1.call-update) | async-done | bytes 114704 | tf_op jit(solution)/shard_map/reduce_scatter | solution.py:47
  523.7 23.4 %reduce-scatter.7.cloned.1.call-done = bf16[1,56,2,512]{3,1,2,0:T(8,128)(2,1)} async-done(((bf16[4,56,2,512]{3,1,2,0:T(8,128)(2,1)}), bf16[1,56,2,512]{3,1,2,0:T(8,128)(2,1)}) %reduce-scatter.7.cloned.1.call-update) | async-done | bytes 114704 | tf_op jit(solution)/shard_map/reduce_scatter | solution.py:47
  554.9 8.4 %psum.37 = f32[2,512]{1,0:T(2,128)S(1)} all-reduce(f32[2,512]{1,0:T(2,128)S(1)} %psum.36), channel_id=1, replica_groups=mesh['replica'=2,'fsdp_0'=4,'fsdp_1'=4,'tensor'=4] {'fsdp_0'}, use_global_device_ids=true, to_apply=%region_17.18 | all-reduce | flops 1024 | bytes 8192 | tf_op jit(solution)/shard_map/psum | solution.py:65
  563.4 6.4 %psum.38 = f32[2,512]{1,0:T(2,128)S(1)} all-reduce(f32[2,512]{1,0:T(2,128)S(1)} %psum.37), channel_id=1, replica_groups=mesh['replica'=2,'fsdp_0'=4,'fsdp_1'=4,'tensor'=4] {'fsdp_1'}, use_global_device_ids=true, to_apply=%region_18.19 | all-reduce | flops 1024 | bytes 8192 | tf_op jit(solution)/shard_map/psum | solution.py:65
  569.8 9.2 %psum.39 = f32[2,512]{1,0:T(2,128)S(1)} all-reduce(f32[2,512]{1,0:T(2,128)S(1)} %psum.38), channel_id=1, replica_groups=mesh['replica'=2,'fsdp_0'=4,'fsdp_1'=4,'tensor'=4] {'tensor'}, use_global_device_ids=true, to_apply=%region_19.20 | all-reduce | flops 1024 | bytes 8192 | tf_op jit(solution)/shard_map/psum | solution.py:65
  579.0 24.0 %all-gather.5.cloned.1.call-done = bf16[3584,2,512]{2,0,1:T(8,128)(2,1)} async-done(((bf16[112,2,512]{2,0,1:T(8,128)(2,1)}), bf16[3584,2,512]{2,0,1:T(8,128)(2,1)}) %all-gather.5.cloned.1.call-update) | async-done | bytes 7340048 | tf_op jit(solution)/shard_map/all_gather | solution.py:103
  603.1 8.3 %subtract_convert_fusion = bf16[2,256,3584]{2,1,0:T(8,128)(2,1)} fusion(bf16[2,256,3584]{2,1,0:T(8,128)(2,1)} %copy-done, bf16[3584,2,512]{2,0,1:T(8,128)(2,1)} %all-gather.5.cloned.1.call-done, bf16[2,128,256]{2,1,0:T(8,128)(2,1)S(1)} %convolution_convert_fusion.3, bf16[2,128,256]{2,1,0:T(8,128)(2,1)S(1)} %get-tuple-element.34, ...), kind=kOutput, calls=%fused_computation.5 | convolution fusion | flops 1888485376 | bytes 15204352 | tf_op jit(solution)/shard_map/wmr,cwr->wmc/dot_general | solution.py:106
  (88 shorter events, 63.8 us)
Async XLA Ops:
  7.2 27.1 %all-gather.3.cloned.1.call-start = ((), (), s32[]{:S(2)}) async-start(), calls=%async_computation.5 | async-start | bytes 11010048 | tf_op jit(solution)/shard_map/all_gather | solution.py:69
  7.9 157.0 %all-reduce.3.cloned.1.call-start = ((), (), s32[]{:S(2)}) async-start(), calls=%async_computation.6 | async-start | bytes 2097152 | tf_op jit(solution)/shard_map/psum | solution.py:87
  34.3 5.3 copy-start.6
  40.7 6.5 %copy-start = (bf16[2,256,3584]{2,1,0:T(8,128)(2,1)}, bf16[2,256,3584]{2,1,0:T(8,128)(2,1)S(1)}, u32[]{:S(2)}) copy-start(bf16[2,256,3584]{2,1,0:T(8,128)(2,1)S(1)} %add_convert_fusion) | copy-start | bytes 11010052
  79.1 393.3 %reduce-scatter.9.cloned.1.call-start = ((), (), s32[]{:S(2)}) async-start(), calls=%async_computation.9 | async-start | bytes 2293760 | tf_op jit(solution)/shard_map/reduce_scatter | solution.py:47
  164.9 1.6 copy-start.4
  166.9 1.3 copy-start.3
  329.2 95.7 %copy-start.5 = (f32[2,256,512]{1,2,0:T(8,128)S(1)}, f32[2,256,512]{1,2,0:T(8,128)}, u32[]{:S(2)}) copy-start(f32[2,256,512]{1,2,0:T(8,128)} %copy.72) | copy-start | bytes 3145732
  427.1 4.1 copy-start.1
  444.0 58.6 %reduce-scatter.5.cloned.1.call-start = ((), (), s32[]{:S(2)}) async-start(), calls=%async_computation.7 | async-start | bytes 2293760 | tf_op jit(solution)/shard_map/reduce_scatter | solution.py:47
  445.6 78.1 %reduce-scatter.11.cloned.1.call-start = ((), (), s32[]{:S(2)}) async-start(), calls=%async_computation.10 | async-start | bytes 573440 | tf_op jit(solution)/shard_map/reduce_scatter | solution.py:47
  472.5 74.6 %reduce-scatter.7.cloned.1.call-start = ((), (), s32[]{:S(2)}) async-start(), calls=%async_computation.8 | async-start | bytes 573440 | tf_op jit(solution)/shard_map/reduce_scatter | solution.py:47
  502.7 100.4 %all-gather.5.cloned.1.call-start = ((), (), s32[]{:S(2)}) async-start(), calls=%async_computation.11 | async-start | bytes 7569408 | tf_op jit(solution)/shard_map/all_gather | solution.py:103
  603.1 8.3 %copy-start.2 = (bf16[3584,2,512]{2,0,1:T(8,128)(2,1)S(1)}, bf16[3584,2,512]{2,0,1:T(8,128)(2,1)}, u32[]{:S(2)}) copy-start(bf16[3584,2,512]{2,0,1:T(8,128)(2,1)} %all-gather.5.cloned.1.call-done) | copy-start | bytes 22020100
Sparse Core Ops, SparseCore 0:
  9.6 24.6 all-gather.2
  79.3 85.6 all-reduce.2
  444.2 28.2 reduce-scatter.8
  475.3 27.3 reduce-scatter.4
  504.9 18.7 reduce-scatter.10
  526.0 21.0 reduce-scatter.6
  549.9 53.0 all-gather.4
where the time goes:
time: 632 us; the launch traced here: 627 us
  other arithmetic  249 us (39%)
  waiting for transfers between devices  237 us (38%)
  blocking collectives  59.2 us (9%)
  matrix products  36.4 us (6%)
  local copies, waits for them, and re-layouts  30.5 us (5%)
  between operations  14.7 us (2%)
    another operation x16, other arithmetic, power_step(): factor = jnp.linalg.cholesky(gram_matrix)  154 us
    reduce_scatter x4, waiting for transfers between devices, own_block(): pieces = lax.psum_scatter(pieces, axes[k], scatter_dimension=0, tiled=True)  101 us
    psum x1, waiting for transfers between devices, power_step(): lax.psum(gram_local.astype(jnp.bfloat16), FSDP).astype(jnp.float32)  84.1 us
    another operation x4, other arithmetic, solve_one(): jax.scipy.linalg.solve_triangular(lower_mat, rows_mat.T, lower=True)  81.2 us
    all_to_all x1, blocking collectives, from_everyone(): lax.all_to_all(jnp.broadcast_to(x[None], (size, *x.shape)), axis, 0, 0, t...  30 us
    psum x4, blocking collectives, over_axes(): return functools.reduce(lax.psum, axes, x)  29.2 us
    all_gather x1, waiting for transfers between devices, total_of_pieces(): return lax.all_gather(x, axis).astype(jnp.float32).sum(0)  26.3 us
    all_gather x1, waiting for transfers between devices, power_step(): right_rows = lax.all_gather(back_b, REPLICA_FSDP, axis=0, tiled=True)  24 us
  transfers between devices with their start and end apart: 7, of which 7 were waited for; matrix products, arithmetic and copies ran while one was open for 1% of the time, Pallas kernels for 0%

commit v1 on v0

v1 whole, which is shorter than its diff:
```python
import functools
import math

import jax
import jax.numpy as jnp
from jax import lax
from jax.experimental import pallas as pl
from jax.experimental.pallas import tpu as pltpu
from jax.sharding import Mesh
from jax.sharding import PartitionSpec as P

FEATURES = 4096
UNITS = 14336
RANK = 512
FSDP = ("fsdp_0", "fsdp_1")
MESH = pl.DeviceIdType.MESH
BF16 = jnp.bfloat16
F32 = jnp.float32
ROWS = FEATURES // 16
COLS = UNITS // 4
PIECE = COLS // 16
SLICE = ROWS // 4
STEP = 512
PANEL = 16
BLOCK = 128

momentum_decay = 0.95


def coords():
    return tuple(lax.axis_index(a) for a in ("replica", "fsdp_0", "fsdp_1", "tensor"))


def shifted(i, k):
    return lax.rem(i + k, 4)


class Ring:
    def __init__(self, axis, at, send, recv):
        self.axis, self.at, self.send, self.recv = axis, at, send, recv
        me = lax.axis_index(axis)
        self.me, self.right, self.left, self.far = me, shifted(me, 1), shifted(me, 3), shifted(me, 2)

    def copy(self, k, who, half, to):
        ref = self.at(who, half)
        return pltpu.make_async_remote_copy(
            src_ref=ref,
            dst_ref=ref,
            send_sem=self.send.at[k],
            recv_sem=self.recv.at[k],
            device_id={self.axis: to},
            device_id_type=MESH,
        )

    def start(self):
        self.copy(0, self.me, None, self.right).start()
        self.copy(1, self.me, None, self.left).start()

    def middle(self):
        self.copy(0, self.left, None, self.right).wait_recv()
        self.copy(2, self.left, 0, self.right).start()
        self.copy(1, self.right, None, self.left).wait_recv()
        self.copy(3, self.right, 1, self.left).start()

    def end(self):
        self.copy(2, self.far, 0, self.right).wait_recv()
        self.copy(3, self.far, 1, self.left).wait_recv()

    def drain(self):
        self.copy(0, self.me, None, self.right).wait_send()
        self.copy(1, self.me, None, self.left).wait_send()
        self.copy(2, self.left, 0, self.right).wait_send()
        self.copy(3, self.right, 1, self.left).wait_send()


def rows_of(start, size, half):
    if half is None:
        return pl.ds(start, size)
    return pl.ds(start + half * (size // 2), size // 2)


def projected_rings(full, y, x, z, send, recv):
    parts = ((0, 32, 0, 384), (32, 32, 0, 384), (0, 64, 384, 128))

    def cut(part, half):
        r0, nr, c0, nc = parts[part]
        return rows_of(r0, nr, half), pl.ds(c0, nc)

    every = slice(None)
    plans = (
        (0, 0, "tensor", lambda i: (y, x, i)),
        (0, 1, "fsdp_0", lambda i: (i, x, every)),
        (0, 2, "fsdp_1", lambda i: (every, i, every)),
        (1, 0, "fsdp_1", lambda i: (y, i, z)),
        (1, 1, "tensor", lambda i: (y, every, i)),
        (1, 2, "fsdp_0", lambda i: (i, every, every)),
        (2, 0, "fsdp_0", lambda i: (i, x, z)),
        (2, 1, "fsdp_1", lambda i: (every, i, z)),
        (2, 2, "tensor", lambda i: (every, every, i)),
    )
    phases = ([], [], [])
    for part, phase, axis, where in plans:
        def at(i, half, part=part, where=where):
            return full.at[(*where(i), *cut(part, half))]

        phases[phase].append(Ring(axis, at, send.at[part, phase], recv.at[part, phase]))
    return phases


def blend_kernel(
    grads, momentum, basis, full, turned, blended,
    m_v, g_v, gp_v, b_v, acc, flipped, out_z, in_z,
    load, gs, gr, zs, zr, ags, agr, ts, tr, ps, pr,
):
    r, y, x, z = coords()
    other = 1 - r
    steps = COLS // STEP

    def grad_copy(c, cols):
        return pltpu.make_async_remote_copy(
            src_ref=grads.at[0, other, :, cols],
            dst_ref=gp_v.at[:, cols],
            send_sem=gs.at[c],
            recv_sem=gr.at[c],
            device_id={"replica": other},
            device_id_type=MESH,
        )

    def loads(c, cols):
        return (
            pltpu.make_async_copy(grads.at[0, r, :, cols], g_v.at[:, cols], load.at[0, c]),
            pltpu.make_async_copy(momentum.at[r, :, cols], m_v.at[:, cols], load.at[1, c]),
            pltpu.make_async_copy(basis.at[r, cols, :], b_v.at[cols, :], load.at[2, c]),
        )

    for c in range(steps):
        cols = pl.ds(c * STEP, STEP)
        grad_copy(c, cols).start()
        for copy in loads(c, cols):
            copy.start()
    acc[...] = jnp.zeros_like(acc)

    def blend(c, carry):
        cols = pl.ds(pl.multiple_of(c * STEP, STEP), STEP)
        for copy in loads(c, cols):
            copy.wait()
        grad_copy(c, cols).wait()
        total = g_v[:, cols].astype(F32) + gp_v[:, cols].astype(F32)
        value = (m_v[:, cols].astype(F32) + total).astype(BF16)
        blended[r, :, cols] = value
        flipped[cols, :] = value.T
        acc[...] += jnp.dot(value, b_v[cols, :], preferred_element_type=F32)
        return carry

    lax.fori_loop(0, steps, blend, 0)

    def z_copy(k):
        return pltpu.make_async_remote_copy(
            src_ref=out_z.at[k - 1],
            dst_ref=in_z.at[k - 1],
            send_sem=zs.at[k - 1],
            recv_sem=zr.at[k - 1],
            device_id={"tensor": shifted(z, k)},
            device_id_type=MESH,
        )

    for k in (2, 1, 3):
        rows = pl.ds(pl.multiple_of(shifted(z, k) * SLICE, SLICE), SLICE)
        out_z[k - 1] = acc[rows, :].astype(BF16)
        z_copy(k).start()
    total = acc[pl.ds(pl.multiple_of(z * SLICE, SLICE), SLICE), :]
    for k in (1, 3, 2):
        z_copy(k).wait()
        total = total + in_z[k - 1].astype(F32)
    full[y, x, z] = total.astype(BF16)

    phases = projected_rings(full, y, x, z, ags, agr)
    for phase in phases:
        for ring in phase:
            ring.start()
        for ring in phase:
            ring.middle()
        if phase is not phases[-1]:
            for ring in phase:
                ring.end()

    def turn_copy(k):
        ty, tx = shifted(y, k // 4), shifted(x, k % 4)
        start = pl.multiple_of((ty * 4 + tx) * PIECE, PIECE)
        return pltpu.make_async_remote_copy(
            src_ref=flipped.at[pl.ds(start, PIECE), :],
            dst_ref=turned.at[y, x],
            send_sem=ts.at[k],
            recv_sem=tr.at[k],
            device_id={"fsdp_0": ty, "fsdp_1": tx},
            device_id_type=MESH,
        )

    def turn_arrival(k):
        sy, sx = shifted(y, 4 - k // 4), shifted(x, 4 - k % 4)
        return pltpu.make_async_remote_copy(
            src_ref=turned.at[sy, sx],
            dst_ref=turned.at[sy, sx],
            send_sem=ts.at[k],
            recv_sem=tr.at[k],
            device_id={"fsdp_0": sy, "fsdp_1": sx},
            device_id_type=MESH,
        )

    for k in range(1, 16):
        turn_copy(k).start()
    share = pltpu.make_async_remote_copy(
        src_ref=blended.at[r],
        dst_ref=blended.at[r],
        send_sem=ps.at[0],
        recv_sem=pr.at[0],
        device_id={"replica": other},
        device_id_type=MESH,
    )
    share.start()
    turned[y, x] = flipped[pl.ds(pl.multiple_of((y * 4 + x) * PIECE, PIECE), PIECE), :]
    for ring in phases[-1]:
        ring.end()
    for phase in phases:
        for ring in phase:
            ring.drain()
    for k in range(1, 16):
        turn_copy(k).wait_send()
        turn_arrival(k).wait_recv()
    share.wait_send()
    pltpu.make_async_remote_copy(
        src_ref=blended.at[other],
        dst_ref=blended.at[other],
        send_sem=ps.at[0],
        recv_sem=pr.at[0],
        device_id={"replica": other},
        device_id_type=MESH,
    ).wait_recv()


def halves(value):
    high = value.astype(BF16)
    return high, (value - high.astype(F32)).astype(BF16)


def contract_rows(a, b):
    ah, al = halves(a)
    bh, bl = halves(b)
    return lax.dot_general(
        jnp.concatenate([ah, ah, al], axis=0),
        jnp.concatenate([bh, bl, bh], axis=0),
        (((0,), (0,)), ((), ())),
        preferred_element_type=F32,
    )


def product(a, b):
    ah, al = halves(a)
    bh, bl = halves(b)
    return jnp.dot(
        jnp.concatenate([ah, ah, al], axis=1),
        jnp.concatenate([bh, bl, bh], axis=0),
        preferred_element_type=F32,
    )


def eliminate(work, inverse):
    row = lax.broadcasted_iota(jnp.int32, (PANEL, BLOCK), 0)
    lane = lax.broadcasted_iota(jnp.int32, (BLOCK, BLOCK), 1)

    def panel(p, carry):
        left, right = work[0:PANEL, 0:BLOCK], work[0:PANEL, BLOCK:]
        columns = [jnp.broadcast_to(left[:, k : k + 1], (PANEL, BLOCK)) for k in range(PANEL)]
        inverses = jnp.ones((PANEL, BLOCK), F32)
        for j in range(PANEL):
            inv = 1.0 / columns[j][j : j + 1, :]
            times = jnp.where(row > j, columns[j] * inv, 0.0)
            for k in range(j + 1, PANEL):
                columns[k] = columns[k] - times * columns[k][j : j + 1, :]
            left = left - times * left[j : j + 1, :]
            right = right - times * right[j : j + 1, :]
            inverses = jnp.where(row == j, inv, inverses)
        scale = jnp.sqrt(inverses)
        left, right = left * scale, right * scale
        inverse[pl.ds(pl.multiple_of(p * PANEL, PANEL), PANEL), :] = right
        change = contract_rows(left, jnp.concatenate([left, right], axis=1))
        rest = work[:, 0:BLOCK] - change[:, 0:BLOCK]
        rest = jnp.where(lane < BLOCK - PANEL, pltpu.roll(rest, BLOCK - PANEL, 1), 0.0)
        work[0 : BLOCK - PANEL, 0:BLOCK] = rest[PANEL:, :]
        extra = work[:, BLOCK:] - change[:, BLOCK:]
        work[0 : BLOCK - PANEL, BLOCK:] = extra[PANEL:, :]
        work[BLOCK - PANEL :, :] = jnp.zeros((PANEL, 2 * BLOCK), F32)
        return carry

    lax.fori_loop(0, BLOCK // PANEL, panel, 0)


def factor_inverse(gram, low, work, inverse):
    low[...] = jnp.zeros_like(low)
    count = RANK // BLOCK
    square = (BLOCK, BLOCK)
    eye = jnp.where(
        lax.broadcasted_iota(jnp.int32, square, 0) == lax.broadcasted_iota(jnp.int32, square, 1), 1.0, 0.0
    )
    for k in range(count):
        here, after = slice(k * BLOCK, (k + 1) * BLOCK), slice((k + 1) * BLOCK, RANK)
        work[:, 0:BLOCK] = gram[here, here]
        work[:, BLOCK:] = eye
        eliminate(work, inverse)
        block = inverse[...]
        if k:
            low[here, 0 : k * BLOCK] = product(block, low[here, 0 : k * BLOCK])
        low[here, here] = block
        if k < count - 1:
            upper = product(block, gram[here, after])
            gram[after, after] = gram[after, after] - contract_rows(upper, upper)
            done = slice(0, (k + 1) * BLOCK)
            low[after, done] = low[after, done] - contract_rows(upper, low[here, done])


def basis_kernel(full, turned, own, back, squares, gram, low, work, inverse, total):
    _, y, x, _ = coords()
    gram[...] = jnp.zeros_like(gram)

    def add_gram(b, carry):
        rows = full[b]
        gram[...] += lax.dot_general(rows, rows, (((0,), (0,)), ((), ())), preferred_element_type=F32)
        return carry

    lax.fori_loop(0, 16, add_gram, 0)
    factor_inverse(gram, low, work, inverse)
    high, rest = halves(low[...])
    total[...] = jnp.zeros_like(total)
    dims = (((1,), (1,)), ((), ()))

    def left_rows(b):
        rows = full[b]
        value = lax.dot_general(rows, high, dims, preferred_element_type=F32)
        value += lax.dot_general(rows, rest, dims, preferred_element_type=F32)
        return value.astype(BF16)

    def add_back(b, carry):
        total[...] += jnp.dot(turned[b], left_rows(b), preferred_element_type=F32)
        return carry

    lax.fori_loop(0, 16, add_back, 0)
    own[...] = left_rows(y * 4 + x)
    value = total[...]
    back[...] = value.astype(BF16)
    squares[...] = jnp.sum((value * value).reshape(PIECE // 8, 8, RANK), axis=0)


def gather_kernel(back, squares, own, full, norms, left, sums, s_ag, r_ag, s_n, r_n, s_p, r_p, local):
    r, y, x, z = coords()
    other = 1 - r
    place = (
        pltpu.make_async_copy(back, full.at[r, y, x], local.at[0]),
        pltpu.make_async_copy(own, left.at[r], local.at[1]),
    )
    for copy in place:
        copy.start()

    def sum_copy(phase, axis, k, me):
        return pltpu.make_async_remote_copy(
            src_ref=sums.at[phase, me],
            dst_ref=sums.at[phase, me],
            send_sem=s_n.at[phase, k - 1],
            recv_sem=r_n.at[phase, k - 1],
            device_id={axis: shifted(me, k)},
            device_id_type=MESH,
        )

    def sum_arrival(phase, axis, k, me):
        source = shifted(me, 4 - k)
        return pltpu.make_async_remote_copy(
            src_ref=sums.at[phase, source],
            dst_ref=sums.at[phase, source],
            send_sem=s_n.at[phase, k - 1],
            recv_sem=r_n.at[phase, k - 1],
            device_id={axis: source},
            device_id_type=MESH,
        )

    def send_sums(phase, axis, me, value):
        sums[phase, me] = value
        for k in (2, 1, 3):
            sum_copy(phase, axis, k, me).start()

    def take_sums(phase, axis, me):
        for k in (1, 3, 2):
            sum_arrival(phase, axis, k, me).wait_recv()
        return (sums[phase, 0] + sums[phase, 1]) + (sums[phase, 2] + sums[phase, 3])

    send_sums(0, "tensor", z, squares[...])
    for copy in place:
        copy.wait()

    halfcols = (pl.ds(0, RANK // 2), pl.ds(RANK // 2, RANK // 2))
    every = slice(None)

    def ring(part, phase, axis, where):
        def at(i, half):
            return full.at[(r, *where(i), rows_of(0, PIECE, half), halfcols[part])]

        return Ring(axis, at, s_ag.at[part, phase], r_ag.at[part, phase])

    first = (ring(0, 0, "fsdp_0", lambda i: (i, x)), ring(1, 0, "fsdp_1", lambda i: (y, i)))
    second = (ring(0, 1, "fsdp_1", lambda i: (every, i)), ring(1, 1, "fsdp_0", lambda i: (i, every)))

    def pass_on(k, src):
        return pltpu.make_async_remote_copy(
            src_ref=src,
            dst_ref=src,
            send_sem=s_p.at[k],
            recv_sem=r_p.at[k],
            device_id={"replica": other},
            device_id_type=MESH,
        )

    def group(weight, part, far):
        if part == 0:
            return full.at[weight, :, shifted(x, far), :, halfcols[part]]
        return full.at[weight, shifted(y, far), :, :, halfcols[part]]

    def partner(weight):
        jobs = [(part, far, pass_on(4 * part + far, group(weight, part, far))) for part in (0, 1) for far in range(4)]
        return {(part, far): job for part, far, job in jobs}

    mine, theirs = partner(r), partner(other)
    for g in first:
        g.start()
    pass_on(8, left.at[r]).start()
    for g in first:
        g.middle()
    value = take_sums(0, "tensor", z)
    send_sums(1, "fsdp_1", x, value)
    for g in first:
        g.end()
    for part, g in enumerate(second):
        g.start()
        mine[part, 0].start()
    value = take_sums(1, "fsdp_1", x)
    send_sums(2, "fsdp_0", y, value)
    value = take_sums(2, "fsdp_0", y)
    norms[r] = value
    pass_on(9, norms.at[r]).start()
    for part, g in enumerate(second):
        g.middle()
        mine[part, 1].start()
        mine[part, 3].start()
    for part, g in enumerate(second):
        g.end()
        mine[part, 2].start()
    for g in first + second:
        g.drain()
    for phase, axis, me in ((0, "tensor", z), (1, "fsdp_1", x), (2, "fsdp_0", y)):
        for k in (1, 2, 3):
            sum_copy(phase, axis, k, me).wait_send()
    pass_on(8, left.at[r]).wait_send()
    pass_on(9, norms.at[r]).wait_send()
    pass_on(8, left.at[other]).wait_recv()
    pass_on(9, norms.at[other]).wait_recv()
    for key in mine:
        mine[key].wait_send()
        theirs[key].wait_recv()


def output_kernel(left, back, blended, norms, momentum_new, update, basis_new):
    squares = jnp.sum(norms[0], axis=0, keepdims=True)
    inverse = 1.0 / (jnp.sqrt(squares) + 1e-06)
    rows = back[0]
    normed = (rows.astype(F32) * inverse).astype(BF16)
    basis_new[0] = normed
    dims = (((1,), (1,)), ((), ()))
    feedback = lax.dot_general(left[0], rows, dims, preferred_element_type=F32)
    momentum_new[0] = (blended[0].astype(F32) - (1.0 - momentum_decay) * feedback).astype(BF16)
    scale = math.sqrt(FEATURES * UNITS / RANK)
    update[0] = (scale * lax.dot_general(left[0], normed, dims, preferred_element_type=F32)).astype(BF16)


def shape(dims, dtype=BF16):
    return jax.ShapeDtypeStruct(dims, dtype)


VM = pl.BlockSpec(memory_space=pltpu.VMEM)
ANY = pl.BlockSpec(memory_space=pl.ANY)
DMA = pltpu.SemaphoreType.DMA


def shards(grads, momentum, basis):
    steps = COLS // STEP
    full, turned, blended = pl.pallas_call(
        blend_kernel,
        out_shape=(shape((4, 4, 4, SLICE, RANK)), shape((4, 4, PIECE, ROWS)), shape((2, ROWS, COLS))),
        in_specs=[ANY] * 3,
        out_specs=(VM, VM, VM),
        scratch_shapes=[
            pltpu.VMEM((ROWS, COLS), BF16),
            pltpu.VMEM((ROWS, COLS), BF16),
            pltpu.VMEM((ROWS, COLS), BF16),
            pltpu.VMEM((COLS, RANK), BF16),
            pltpu.VMEM((ROWS, RANK), F32),
            pltpu.VMEM((COLS, ROWS), BF16),
            pltpu.VMEM((3, SLICE, RANK), BF16),
            pltpu.VMEM((3, SLICE, RANK), BF16),
            DMA((3, steps)),
            DMA((steps,)),
            DMA((steps,)),
            DMA((3,)),
            DMA((3,)),
            DMA((3, 3, 4)),
            DMA((3, 3, 4)),
            DMA((16,)),
            DMA((16,)),
            DMA((1,)),
            DMA((1,)),
        ],
        compiler_params=pltpu.CompilerParams(has_side_effects=True),
        name="blend",
    )(grads, momentum, basis)
    own, back, squares = pl.pallas_call(
        basis_kernel,
        out_shape=(shape((ROWS, RANK)), shape((PIECE, RANK)), shape((8, RANK), F32)),
        in_specs=[VM] * 2,
        out_specs=(VM, VM, VM),
        scratch_shapes=[
            pltpu.VMEM((RANK, RANK), F32),
            pltpu.VMEM((RANK, RANK), F32),
            pltpu.VMEM((BLOCK, 2 * BLOCK), F32),
            pltpu.VMEM((BLOCK, BLOCK), F32),
            pltpu.VMEM((PIECE, RANK), F32),
        ],
        name="left_basis",
    )(full.reshape(16, ROWS, RANK), turned.reshape(16, PIECE, ROWS))
    gathered, norms, left = pl.pallas_call(
        gather_kernel,
        out_shape=(shape((2, 4, 4, PIECE, RANK)), shape((2, 8, RANK), F32), shape((2, ROWS, RANK))),
        in_specs=[VM] * 3,
        out_specs=(VM, VM, VM),
        scratch_shapes=[
            pltpu.VMEM((3, 4, 8, RANK), F32),
            DMA((2, 2, 4)),
            DMA((2, 2, 4)),
            DMA((3, 3)),
            DMA((3, 3)),
            DMA((10,)),
            DMA((10,)),
            DMA((2,)),
        ],
        compiler_params=pltpu.CompilerParams(has_side_effects=True),
        name="gather",
    )(back, squares, own)
    wide = COLS // 4
    return pl.pallas_call(
        output_kernel,
        out_shape=(shape((2, ROWS, COLS)), shape((2, ROWS, COLS)), shape((2, COLS, RANK))),
        grid=(2, 4),
        in_specs=[
            pl.BlockSpec((1, ROWS, RANK), lambda w, c: (w, 0, 0)),
            pl.BlockSpec((1, wide, RANK), lambda w, c: (w, c, 0)),
            pl.BlockSpec((1, ROWS, wide), lambda w, c: (w, 0, c)),
            pl.BlockSpec((1, 8, RANK), lambda w, c: (w, 0, 0)),
        ],
        out_specs=(
            pl.BlockSpec((1, ROWS, wide), lambda w, c: (w, 0, c)),
            pl.BlockSpec((1, ROWS, wide), lambda w, c: (w, 0, c)),
            pl.BlockSpec((1, wide, RANK), lambda w, c: (w, c, 0)),
        ),
        name="outputs",
    )(left, gathered.reshape(2, COLS, RANK), blended, norms)


def solution(mesh):
    torus = Mesh(
        mesh.devices.reshape(mesh.shape["replica"], 4, 4, mesh.shape["tensor"]),
        ("replica", "fsdp_0", "fsdp_1", "tensor"),
    )
    return jax.shard_map(
        shards,
        mesh=torus,
        in_specs=(
            P("replica", None, FSDP, "tensor"),
            P(None, FSDP, "tensor"),
            P(None, "tensor", None),
        ),
        out_specs=(P(None, FSDP, "tensor"), P(None, FSDP, "tensor"), P(None, "tensor", None)),
        check_vma=False,
    )
```

time: 632 us -> 175 us (0.28)
  other arithmetic: 249 us -> 0 us
  waiting for transfers between devices: 237 us -> 0 us
  Pallas kernels: 0 us -> 174 us
  blocking collectives: 59.2 us -> 0 us
  matrix products: 36.4 us -> 0 us
  local copies, waits for them, and re-layouts: 30.5 us -> 0 us
  between operations: 14.7 us -> 0.65 us
    another operation x20 -> x0, other arithmetic: 235 us -> none  [the longest x16 154 us: power_step(): factor = jnp.linalg.cholesky(gram_matrix)]
    pallas_call x0 -> x4, Pallas kernels: none -> 174 us  [the longest x1 72.6 us: shards(): pl.pallas_call(blend_kernel, out_shape=(shape((4, 4, 4, SLICE, RANK)), sh...]
    reduce_scatter x4 -> x0, waiting for transfers between devices: 101 us -> none  [own_block(): pieces = lax.psum_scatter(pieces, axes[k], scatter_dimension=0, tiled=True)]
    psum x1 -> x0, waiting for transfers between devices: 84.1 us -> none  [power_step(): lax.psum(gram_local.astype(jnp.bfloat16), FSDP).astype(jnp.float32)]
    all_gather x2 -> x0, waiting for transfers between devices: 50.4 us -> none  [the longest x1 26.3 us: total_of_pieces(): return lax.all_gather(x, axis).astype(jnp.float32).sum(0)]
    all_to_all x1 -> x0, blocking collectives: 30 us -> none  [from_everyone(): lax.all_to_all(jnp.broadcast_to(x[None], (size, *x.shape)), axis, 0, 0, t...]
    psum x4 -> x0, blocking collectives: 29.2 us -> none  [over_axes(): return functools.reduce(lax.psum, axes, x)]
    dot_general x5 -> x0, matrix products: 23.5 us -> none  [the longest x1 8.33 us: power_step(): jnp.einsum('wmr,cwr->wmc', left_basis, right_rows, preferred_element_type...]
  transfers between devices with their start and end apart: 7 -> 0, of which waited for: 7 -> 0; matrix products, arithmetic and copies ran while one was open for 1% -> 0% of each run, Pallas kernels for 0% -> 0%
where the time goes in v1:
time: 175 us; the launch traced here: 174 us
  Pallas kernels  174 us (99%)
    pallas_call x1, Pallas kernels, shards(): pl.pallas_call(blend_kernel, out_shape=(shape((4, 4, 4, SLICE, RANK)), sh...  72.6 us
    pallas_call x1, Pallas kernels, shards(): pl.pallas_call(gather_kernel, out_shape=(shape((2, 4, 4, PIECE, RANK)), s...  48 us
    pallas_call x1, Pallas kernels, shards(): pl.pallas_call(basis_kernel, out_shape=(shape((ROWS, RANK)), shape((PIECE...  39.3 us
    pallas_call x1, Pallas kernels, shards(): pl.pallas_call(output_kernel, out_shape=(shape((2, ROWS, COLS)), shape((2...  13.7 us

profile of v1, /device:TPU:1, one launch (start us, length us, event | category | flops | bytes accessed | tf_op | source)
XLA Modules:
  0.0 174.2 jit_solution(17682463373682995330)
XLA Ops:
  0.6 72.6 %blend.1 = (bf16[4,4,4,64,512]{4,3,2,1,0:T(8,128)(2,1)}, bf16[4,4,224,256]{3,2,1,0:T(8,128)(2,1)}, bf16[2,256,3584]{2,1,0:T(8,128)(2,1)}) custom-call(bf16[1,2,256,3584]{3,2,1,0:T(8,128)(2,1)} %grads.1, bf16[2,256,3584]{2,1,0:T(8,128)(2,1)} %momentum.1, bf16[2,3584,512]{2,1,0:T(8,128)(2,1)} %basis.1), custom_call_target="tpu_custom_call" | custom-call | tf_op jit(solution)/shard_map/blend/pallas_call | solution.py:492
  73.2 39.3 %left_basis.1 = (bf16[256,512]{1,0:T(8,128)(2,1)}, bf16[224,512]{1,0:T(8,128)(2,1)}, f32[8,512]{1,0:T(8,128)}) custom-call(bf16[16,256,512]{2,1,0:T(8,128)(2,1)} %bitcast.4, bf16[16,224,256]{2,1,0:T(8,128)(2,1)} %bitcast.5), custom_call_target="tpu_custom_call" | custom-call | tf_op jit(solution)/shard_map/left_basis/pallas_call | solution.py:521
  112.6 48.0 %gather.1 = (bf16[2,4,4,224,512]{4,3,2,1,0:T(8,128)(2,1)}, f32[2,8,512]{2,1,0:T(8,128)}, bf16[2,256,512]{2,1,0:T(8,128)(2,1)}) custom-call(bf16[224,512]{1,0:T(8,128)(2,1)} %get-tuple-element.14.back, f32[8,512]{1,0:T(8,128)} %get-tuple-element.15.squares, bf16[256,512]{1,0:T(8,128)(2,1)} %get-tuple-element.16.own), custom_call_target="tpu_custom_call" | custom-call | tf_op jit(solution)/shard_map/gather/pallas_call | solution.py:535
  160.5 13.7 %outputs.1 = (bf16[2,256,3584]{2,1,0:T(8,128)(2,1)}, bf16[2,256,3584]{2,1,0:T(8,128)(2,1)}, bf16[2,3584,512]{2,1,0:T(8,128)(2,1)}) custom-call(bf16[2,256,512]{2,1,0:T(8,128)(2,1)} %get-tuple-element.17.left, bf16[2,3584,512]{2,1,0:T(8,128)(2,1)} %bitcast.3, bf16[2,256,3584]{2,1,0:T(8,128)(2,1)} %get-tuple-element.19.blended, ...), custom_call_target="tpu_custom_call" | custom-call | tf_op jit(solution)/shard_map/outputs/pallas_call | solution.py:554

commit v2 on v1

v2 whole, which is shorter than its diff:
```python
import functools
import math

import jax
import jax.numpy as jnp
from jax import lax
from jax.experimental import pallas as pl
from jax.experimental.pallas import tpu as pltpu
from jax.sharding import Mesh
from jax.sharding import PartitionSpec as P

FEATURES = 4096
UNITS = 14336
RANK = 512
FSDP = ("fsdp_0", "fsdp_1")
MESH = pl.DeviceIdType.MESH
BF16 = jnp.bfloat16
F32 = jnp.float32
ROWS = FEATURES // 16
COLS = UNITS // 4
PIECE = COLS // 16
SLICE = ROWS // 4
STEP = 512
PANEL = 16
BLOCK = 128

momentum_decay = 0.95


def coords():
    return tuple(lax.axis_index(a) for a in ("replica", "fsdp_0", "fsdp_1", "tensor"))


def shifted(i, k):
    return lax.rem(i + k, 4)


class Ring:
    def __init__(self, axis, at, send, recv):
        self.axis, self.at, self.send, self.recv = axis, at, send, recv
        me = lax.axis_index(axis)
        self.me, self.right, self.left, self.far = me, shifted(me, 1), shifted(me, 3), shifted(me, 2)

    def copy(self, k, who, half, to):
        ref = self.at(who, half)
        return pltpu.make_async_remote_copy(
            src_ref=ref,
            dst_ref=ref,
            send_sem=self.send.at[k],
            recv_sem=self.recv.at[k],
            device_id={self.axis: to},
            device_id_type=MESH,
        )

    def start(self):
        self.copy(0, self.me, None, self.right).start()
        self.copy(1, self.me, None, self.left).start()

    def middle(self):
        self.copy(0, self.left, None, self.right).wait_recv()
        self.copy(2, self.left, 0, self.right).start()
        self.copy(1, self.right, None, self.left).wait_recv()
        self.copy(3, self.right, 1, self.left).start()

    def end(self):
        self.copy(2, self.far, 0, self.right).wait_recv()
        self.copy(3, self.far, 1, self.left).wait_recv()

    def drain(self):
        self.copy(0, self.me, None, self.right).wait_send()
        self.copy(1, self.me, None, self.left).wait_send()
        self.copy(2, self.left, 0, self.right).wait_send()
        self.copy(3, self.right, 1, self.left).wait_send()


def rows_of(start, size, half):
    if half is None:
        return pl.ds(start, size)
    return pl.ds(start + half * (size // 2), size // 2)


def projected_rings(full, y, x, z, send, recv):
    parts = ((0, 32, 0, 384), (32, 32, 0, 384), (0, 64, 384, 128))

    def cut(part, half):
        r0, nr, c0, nc = parts[part]
        return rows_of(r0, nr, half), pl.ds(c0, nc)

    every = slice(None)
    plans = (
        (0, 0, "tensor", lambda i: (y, x, i)),
        (0, 1, "fsdp_0", lambda i: (i, x, every)),
        (0, 2, "fsdp_1", lambda i: (every, i, every)),
        (1, 0, "fsdp_1", lambda i: (y, i, z)),
        (1, 1, "tensor", lambda i: (y, every, i)),
        (1, 2, "fsdp_0", lambda i: (i, every, every)),
        (2, 0, "fsdp_0", lambda i: (i, x, z)),
        (2, 1, "fsdp_1", lambda i: (every, i, z)),
        (2, 2, "tensor", lambda i: (every, every, i)),
    )
    phases = ([], [], [])
    for part, phase, axis, where in plans:
        def at(i, half, part=part, where=where):
            return full.at[(*where(i), *cut(part, half))]

        phases[phase].append(Ring(axis, at, send.at[part, phase], recv.at[part, phase]))
    return phases


class Spread:
    def __init__(self, part, r, y, x, held, out, send, recv, store):
        self.part, self.r, self.held, self.out, self.store = part, r, held, out, store
        self.send, self.recv = send.at[part], recv.at[part]
        self.line_axis, self.side_axis = ("fsdp_0", "fsdp_1") if part == 0 else ("fsdp_1", "fsdp_0")
        self.a, self.b = (y, x) if part == 0 else (x, y)
        self.sent = []
        self.stored = []

    def ref(self, o, q, half=None):
        i, j = shifted(self.a, o), shifted(self.b, q)
        place = (i, j) if self.part == 0 else (j, i)
        return (*place, rows_of(0, PIECE, half), pl.ds(self.part * (RANK // 2), RANK // 2))

    def copy(self, k, o, q, axis, way, half=None):
        ref = self.held.at[self.ref(o, q, half)]
        return pltpu.make_async_remote_copy(
            src_ref=ref,
            dst_ref=ref,
            send_sem=self.send.at[k],
            recv_sem=self.recv.at[k],
            device_id={axis: shifted(lax.axis_index(axis), way)},
            device_id_type=MESH,
        )

    def go(self, *args):
        copy = self.copy(*args)
        copy.start()
        self.sent.append(copy)

    def hand_over(self, o, q):
        k = 16 + 4 * o + q
        ref = self.ref(o, q)
        copy = pltpu.make_async_remote_copy(
            src_ref=self.held.at[ref],
            dst_ref=self.out.at[(self.r, *ref)],
            send_sem=self.send.at[k],
            recv_sem=self.recv.at[k],
            device_id={"replica": 1 - self.r},
            device_id_type=MESH,
        )
        copy.start()
        self.sent.append(copy)
        kept = pltpu.make_async_copy(
            self.held.at[ref], self.out.at[(self.r, *ref)], self.store.at[3 + 16 * self.part + 4 * o + q]
        )
        kept.start()
        self.stored.append(kept)

    def begin(self):
        self.go(0, 0, 0, self.line_axis, 1)
        self.go(1, 0, 0, self.line_axis, 3)
        self.sides(0)
        self.hand_over(0, 0)

    def sides(self, o):
        self.go(4 + o, o, 0, self.side_axis, 1)
        self.go(8 + o, o, 0, self.side_axis, 3)

    def line(self, o):
        if o == 3:
            self.copy(0, 3, 0, self.line_axis, 1).wait_recv()
            self.go(2, 3, 0, self.line_axis, 1, 0)
        elif o == 1:
            self.copy(1, 1, 0, self.line_axis, 3).wait_recv()
            self.go(3, 1, 0, self.line_axis, 3, 1)
        else:
            self.copy(2, 2, 0, self.line_axis, 1, 0).wait_recv()
            self.copy(3, 2, 0, self.line_axis, 3, 1).wait_recv()
        self.sides(o)
        self.hand_over(o, 0)

    def side(self, o):
        first, second = ((3, 1) if o in (0, 3) else (1, 3))
        for q in (first, second):
            if q == 3:
                self.copy(4 + o, o, 3, self.side_axis, 1).wait_recv()
            else:
                self.copy(8 + o, o, 1, self.side_axis, 3).wait_recv()
            if q == first:
                self.go(12 + o, o, q, self.side_axis, 4 - q)
            self.hand_over(o, q)

    def last(self, o):
        self.copy(12 + o, o, 2, self.side_axis, 1 if o in (0, 3) else 3).wait_recv()
        self.hand_over(o, 2)

    def drain(self):
        for copy in self.sent:
            copy.wait_send()
        for copy in self.stored:
            copy.wait()
        for o in range(4):
            for q in range(4):
                k = 16 + 4 * o + q
                ref = self.out.at[(1 - self.r, *self.ref(o, q))]
                pltpu.make_async_remote_copy(
                    src_ref=ref,
                    dst_ref=ref,
                    send_sem=self.send.at[k],
                    recv_sem=self.recv.at[k],
                    device_id={"replica": 1 - self.r},
                    device_id_type=MESH,
                ).wait_recv()


def halves(value):
    high = value.astype(BF16)
    return high, (value - high.astype(F32)).astype(BF16)


def contract_rows(a, b):
    ah, al = halves(a)
    bh, bl = halves(b)
    return lax.dot_general(
        jnp.concatenate([ah, ah, al], axis=0),
        jnp.concatenate([bh, bl, bh], axis=0),
        (((0,), (0,)), ((), ())),
        preferred_element_type=F32,
    )


def product(a, b):
    ah, al = halves(a)
    bh, bl = halves(b)
    return jnp.dot(
        jnp.concatenate([ah, ah, al], axis=1),
        jnp.concatenate([bh, bl, bh], axis=0),
        preferred_element_type=F32,
    )


def eliminate(work, inverse):
    row = lax.broadcasted_iota(jnp.int32, (PANEL, BLOCK), 0)
    lane = lax.broadcasted_iota(jnp.int32, (BLOCK, BLOCK), 1)

    def panel(p, carry):
        left, right = work[0:PANEL, 0:BLOCK], work[0:PANEL, BLOCK:]
        columns = [jnp.broadcast_to(left[:, k : k + 1], (PANEL, BLOCK)) for k in range(PANEL)]
        inverses = jnp.ones((PANEL, BLOCK), F32)
        for j in range(PANEL):
            inv = 1.0 / columns[j][j : j + 1, :]
            times = jnp.where(row > j, columns[j] * inv, 0.0)
            for k in range(j + 1, PANEL):
                columns[k] = columns[k] - times * columns[k][j : j + 1, :]
            left = left - times * left[j : j + 1, :]
            right = right - times * right[j : j + 1, :]
            inverses = jnp.where(row == j, inv, inverses)
        scale = jnp.sqrt(inverses)
        left, right = left * scale, right * scale
        inverse[pl.ds(pl.multiple_of(p * PANEL, PANEL), PANEL), :] = right
        change = contract_rows(left, jnp.concatenate([left, right], axis=1))
        rest = work[:, 0:BLOCK] - change[:, 0:BLOCK]
        rest = jnp.where(lane < BLOCK - PANEL, pltpu.roll(rest, BLOCK - PANEL, 1), 0.0)
        work[0 : BLOCK - PANEL, 0:BLOCK] = rest[PANEL:, :]
        extra = work[:, BLOCK:] - change[:, BLOCK:]
        work[0 : BLOCK - PANEL, BLOCK:] = extra[PANEL:, :]
        work[BLOCK - PANEL :, :] = jnp.zeros((PANEL, 2 * BLOCK), F32)
        return carry

    lax.fori_loop(0, BLOCK // PANEL, panel, 0)


def factor_inverse(gram, low, work, inverse):
    low[...] = jnp.zeros_like(low)
    count = RANK // BLOCK
    square = (BLOCK, BLOCK)
    eye = jnp.where(
        lax.broadcasted_iota(jnp.int32, square, 0) == lax.broadcasted_iota(jnp.int32, square, 1), 1.0, 0.0
    )
    for k in range(count):
        here, after = slice(k * BLOCK, (k + 1) * BLOCK), slice((k + 1) * BLOCK, RANK)
        work[:, 0:BLOCK] = gram[here, here]
        work[:, BLOCK:] = eye
        eliminate(work, inverse)
        block = inverse[...]
        if k:
            low[here, 0 : k * BLOCK] = product(block, low[here, 0 : k * BLOCK])
        low[here, here] = block
        if k < count - 1:
            upper = product(block, gram[here, after])
            gram[after, after] = gram[after, after] - contract_rows(upper, upper)
            done = slice(0, (k + 1) * BLOCK)
            low[after, done] = low[after, done] - contract_rows(upper, low[here, done])


def step_kernel(
    grads, momentum, basis, blended, gathered, norms, left,
    m_v, g_v, gp_v, b_v, acc, flipped, out_z, in_z, full, turned, gram, low, work, inverse, total, own, rows_v, sums,
    load, gs, gr, zs, zr, ags, agr, ts, tr, bs, br, s_n, r_n, s_p, r_p, store,
):
    r, y, x, z = coords()
    other = 1 - r
    steps = COLS // STEP

    def grad_copy(c, cols):
        return pltpu.make_async_remote_copy(
            src_ref=grads.at[0, other, :, cols],
            dst_ref=gp_v.at[:, cols],
            send_sem=gs.at[c],
            recv_sem=gr.at[c],
            device_id={"replica": other},
            device_id_type=MESH,
        )

    def loads(c, cols):
        return (
            pltpu.make_async_copy(grads.at[0, r, :, cols], g_v.at[:, cols], load.at[0, c]),
            pltpu.make_async_copy(momentum.at[r, :, cols], m_v.at[:, cols], load.at[1, c]),
            pltpu.make_async_copy(basis.at[r, cols, :], b_v.at[cols, :], load.at[2, c]),
        )

    for c in range(steps):
        cols = pl.ds(c * STEP, STEP)
        grad_copy(c, cols).start()
        for copy in loads(c, cols):
            copy.start()
    acc[...] = jnp.zeros_like(acc)

    def blend(c, carry):
        cols = pl.ds(pl.multiple_of(c * STEP, STEP), STEP)
        for copy in loads(c, cols):
            copy.wait()
        grad_copy(c, cols).wait()
        both = g_v[:, cols].astype(F32) + gp_v[:, cols].astype(F32)
        value = (m_v[:, cols].astype(F32) + both).astype(BF16)
        m_v[:, cols] = value
        acc[...] += jnp.dot(value, b_v[cols, :], preferred_element_type=F32)
        return carry

    lax.fori_loop(0, steps, blend, 0)

    def z_copy(k):
        return pltpu.make_async_remote_copy(
            src_ref=out_z.at[k - 1],
            dst_ref=in_z.at[k - 1],
            send_sem=zs.at[k - 1],
            recv_sem=zr.at[k - 1],
            device_id={"tensor": shifted(z, k)},
            device_id_type=MESH,
        )

    for k in (2, 1, 3):
        rows = pl.ds(pl.multiple_of(shifted(z, k) * SLICE, SLICE), SLICE)
        out_z[k - 1] = acc[rows, :].astype(BF16)
        z_copy(k).start()

    def flip(c, carry):
        cols = pl.ds(pl.multiple_of(c * STEP, STEP), STEP)
        flipped[cols, :] = m_v[:, cols].T
        return carry

    lax.fori_loop(0, steps, flip, 0)
    piece = acc[pl.ds(pl.multiple_of(z * SLICE, SLICE), SLICE), :]
    for k in (1, 3, 2):
        z_copy(k).wait()
        piece = piece + in_z[k - 1].astype(F32)
    full[y, x, z] = piece.astype(BF16)

    phases = projected_rings(full, y, x, z, ags, agr)
    for phase in phases:
        for ring in phase:
            ring.start()
        for ring in phase:
            ring.middle()
        if phase is not phases[-1]:
            for ring in phase:
                ring.end()

    def turn_copy(k):
        ty, tx = shifted(y, k // 4), shifted(x, k % 4)
        start = pl.multiple_of((ty * 4 + tx) * PIECE, PIECE)
        return pltpu.make_async_remote_copy(
            src_ref=flipped.at[pl.ds(start, PIECE), :],
            dst_ref=turned.at[y, x],
            send_sem=ts.at[k],
            recv_sem=tr.at[k],
            device_id={"fsdp_0": ty, "fsdp_1": tx},
            device_id_type=MESH,
        )

    def turn_arrival(k):
        sy, sx = shifted(y, 4 - k // 4), shifted(x, 4 - k % 4)
        return pltpu.make_async_remote_copy(
            src_ref=turned.at[sy, sx],
            dst_ref=turned.at[sy, sx],
            send_sem=ts.at[k],
            recv_sem=tr.at[k],
            device_id={"fsdp_0": sy, "fsdp_1": sx},
            device_id_type=MESH,
        )

    for k in range(1, 16):
        turn_copy(k).start()

    def to_partner(src, dst, send, recv):
        return pltpu.make_async_remote_copy(
            src_ref=src,
            dst_ref=dst,
            send_sem=send,
            recv_sem=recv,
            device_id={"replica": other},
            device_id_type=MESH,
        )

    share = to_partner(m_v, blended.at[r], bs.at[0], br.at[0])
    share.start()
    keep = pltpu.make_async_copy(m_v, blended.at[r], store.at[0])
    keep.start()
    turned[y, x] = flipped[pl.ds(pl.multiple_of((y * 4 + x) * PIECE, PIECE), PIECE), :]
    for ring in phases[-1]:
        ring.end()

    gram[...] = jnp.zeros_like(gram)

    def add_gram(b, carry):
        rows = full[b // 4, lax.rem(b, 4)].reshape(ROWS, RANK)
        gram[...] += lax.dot_general(rows, rows, (((0,), (0,)), ((), ())), preferred_element_type=F32)
        return carry

    lax.fori_loop(0, 16, add_gram, 0)
    factor_inverse(gram, low, work, inverse)
    high = low[...].astype(BF16)
    total[...] = jnp.zeros_like(total)
    dims = (((1,), (1,)), ((), ()))

    def left_rows(by, bx):
        rows = full[by, bx].reshape(ROWS, RANK)
        return lax.dot_general(rows, high, dims, preferred_element_type=F32).astype(BF16)

    own[...] = left_rows(y, x)
    keep_left = pltpu.make_async_copy(own, left.at[r], store.at[1])
    keep_left.start()
    share_left = to_partner(own, left.at[r], bs.at[1], br.at[1])
    share_left.start()
    for k in range(1, 16):
        turn_copy(k).wait_send()
        turn_arrival(k).wait_recv()

    def add_back(b, carry):
        by, bx = b // 4, lax.rem(b, 4)
        total[...] += jnp.dot(turned[by, bx], left_rows(by, bx), preferred_element_type=F32)
        return carry

    lax.fori_loop(0, 16, add_back, 0)
    value = total[...]
    rows_v[y, x] = value.astype(BF16)

    def sum_copy(phase, axis, k, me):
        return pltpu.make_async_remote_copy(
            src_ref=sums.at[phase, me],
            dst_ref=sums.at[phase, me],
            send_sem=s_n.at[phase, k - 1],
            recv_sem=r_n.at[phase, k - 1],
            device_id={axis: shifted(me, k)},
            device_id_type=MESH,
        )

    def sum_arrival(phase, axis, k, me):
        source = shifted(me, 4 - k)
        return pltpu.make_async_remote_copy(
            src_ref=sums.at[phase, source],
            dst_ref=sums.at[phase, source],
            send_sem=s_n.at[phase, k - 1],
            recv_sem=r_n.at[phase, k - 1],
            device_id={axis: source},
            device_id_type=MESH,
        )

    def send_sums(phase, axis, me, block):
        sums[phase, me] = block
        for k in (2, 1, 3):
            sum_copy(phase, axis, k, me).start()

    def take_sums(phase, axis, me):
        for k in (1, 3, 2):
            sum_arrival(phase, axis, k, me).wait_recv()
        return (sums[phase, 0] + sums[phase, 1]) + (sums[phase, 2] + sums[phase, 3])

    spreads = (Spread(0, r, y, x, rows_v, gathered, s_p, r_p, store), Spread(1, r, y, x, rows_v, gathered, s_p, r_p, store))

    def both(job, *args):
        for spread in spreads:
            getattr(spread, job)(*args)

    both("begin")
    send_sums(0, "tensor", z, jnp.sum((value * value).reshape(PIECE // 8, 8, RANK), axis=0))
    both("line", 3)
    both("line", 1)
    part_sums = take_sums(0, "tensor", z)
    send_sums(1, "fsdp_1", x, part_sums)
    both("side", 0)
    both("line", 2)
    both("side", 3)
    part_sums = take_sums(1, "fsdp_1", x)
    send_sums(2, "fsdp_0", y, part_sums)
    both("side", 1)
    part_sums = take_sums(2, "fsdp_0", y)
    sums[3, 0] = part_sums
    keep_norms = pltpu.make_async_copy(sums.at[3, 0], norms.at[r], store.at[2])
    keep_norms.start()
    share_norms = to_partner(sums.at[3, 0], norms.at[r], bs.at[2], br.at[2])
    share_norms.start()
    both("side", 2)
    for sub in (0, 3, 1, 2):
        both("last", sub)
    both("drain")
    for ring in phases[0] + phases[1] + phases[2]:
        ring.drain()
    for phase, axis, me in ((0, "tensor", z), (1, "fsdp_1", x), (2, "fsdp_0", y)):
        for k in (1, 2, 3):
            sum_copy(phase, axis, k, me).wait_send()
    for copy in (keep, keep_left, keep_norms):
        copy.wait()
    for copy in (share, share_left, share_norms):
        copy.wait_send()
    for k, out in enumerate((blended, left, norms)):
        to_partner(out.at[other], out.at[other], bs.at[k], br.at[k]).wait_recv()


def output_kernel(left, back, blended, norms, momentum_new, update, basis_new):
    squares = jnp.sum(norms[0], axis=0, keepdims=True)
    inverse = 1.0 / (jnp.sqrt(squares) + 1e-06)
    rows = back[0]
    normed = (rows.astype(F32) * inverse).astype(BF16)
    basis_new[0] = normed
    dims = (((1,), (1,)), ((), ()))
    feedback = lax.dot_general(left[0], rows, dims, preferred_element_type=F32)
    momentum_new[0] = (blended[0].astype(F32) - (1.0 - momentum_decay) * feedback).astype(BF16)
    scale = math.sqrt(FEATURES * UNITS / RANK)
    update[0] = (scale * lax.dot_general(left[0], normed, dims, preferred_element_type=F32)).astype(BF16)


def shape(dims, dtype=BF16):
    return jax.ShapeDtypeStruct(dims, dtype)


VM = pl.BlockSpec(memory_space=pltpu.VMEM)
ANY = pl.BlockSpec(memory_space=pl.ANY)
DMA = pltpu.SemaphoreType.DMA


def shards(grads, momentum, basis):
    steps = COLS // STEP
    blended, gathered, norms, left = pl.pallas_call(
        step_kernel,
        out_shape=(
            shape((2, ROWS, COLS)),
            shape((2, 4, 4, PIECE, RANK)),
            shape((2, 8, RANK), F32),
            shape((2, ROWS, RANK)),
        ),
        in_specs=[ANY] * 3,
        out_specs=(ANY,) * 4,
        scratch_shapes=[
            pltpu.VMEM((ROWS, COLS), BF16),
            pltpu.VMEM((ROWS, COLS), BF16),
            pltpu.VMEM((ROWS, COLS), BF16),
            pltpu.VMEM((COLS, RANK), BF16),
            pltpu.VMEM((ROWS, RANK), F32),
            pltpu.VMEM((COLS, ROWS), BF16),
            pltpu.VMEM((3, SLICE, RANK), BF16),
            pltpu.VMEM((3, SLICE, RANK), BF16),
            pltpu.VMEM((4, 4, 4, SLICE, RANK), BF16),
            pltpu.VMEM((4, 4, PIECE, ROWS), BF16),
            pltpu.VMEM((RANK, RANK), F32),
            pltpu.VMEM((RANK, RANK), F32),
            pltpu.VMEM((BLOCK, 2 * BLOCK), F32),
            pltpu.VMEM((BLOCK, BLOCK), F32),
            pltpu.VMEM((PIECE, RANK), F32),
            pltpu.VMEM((ROWS, RANK), BF16),
            pltpu.VMEM((4, 4, PIECE, RANK), BF16),
            pltpu.VMEM((4, 4, 8, RANK), F32),
            DMA((3, steps)),
            DMA((steps,)),
            DMA((steps,)),
            DMA((3,)),
            DMA((3,)),
            DMA((3, 3, 4)),
            DMA((3, 3, 4)),
            DMA((16,)),
            DMA((16,)),
            DMA((3,)),
            DMA((3,)),
            DMA((3, 3)),
            DMA((3, 3)),
            DMA((2, 32)),
            DMA((2, 32)),
            DMA((35,)),
        ],
        compiler_params=pltpu.CompilerParams(has_side_effects=True),
        name="step",
    )(grads, momentum, basis)
    wide = COLS // 4
    return pl.pallas_call(
        output_kernel,
        out_shape=(shape((2, ROWS, COLS)), shape((2, ROWS, COLS)), shape((2, COLS, RANK))),
        grid=(2, 4),
        in_specs=[
            pl.BlockSpec((1, ROWS, RANK), lambda w, c: (w, 0, 0)),
            pl.BlockSpec((1, wide, RANK), lambda w, c: (w, c, 0)),
            pl.BlockSpec((1, ROWS, wide), lambda w, c: (w, 0, c)),
            pl.BlockSpec((1, 8, RANK), lambda w, c: (w, 0, 0)),
        ],
        out_specs=(
            pl.BlockSpec((1, ROWS, wide), lambda w, c: (w, 0, c)),
            pl.BlockSpec((1, ROWS, wide), lambda w, c: (w, 0, c)),
            pl.BlockSpec((1, wide, RANK), lambda w, c: (w, c, 0)),
        ),
        name="outputs",
    )(left, gathered.reshape(2, COLS, RANK), blended, norms)


def solution(mesh):
    torus = Mesh(
        mesh.devices.reshape(mesh.shape["replica"], 4, 4, mesh.shape["tensor"]),
        ("replica", "fsdp_0", "fsdp_1", "tensor"),
    )
    return jax.shard_map(
        shards,
        mesh=torus,
        in_specs=(
            P("replica", None, FSDP, "tensor"),
            P(None, FSDP, "tensor"),
            P(None, "tensor", None),
        ),
        out_specs=(P(None, FSDP, "tensor"), P(None, FSDP, "tensor"), P(None, "tensor", None)),
        check_vma=False,
    )
```

time: 175 us -> 136 us (0.78)
  Pallas kernels: 174 us -> 135 us
    pallas_call x3 -> x1, Pallas kernels: 160 us -> 121 us  [shards(): pl.pallas_call(step_kernel, out_shape=(shape((2, ROWS, COLS)), shape((2,...]
where the time goes in v2:
time: 136 us; the launch traced here: 135 us
  Pallas kernels  135 us (99%)
    pallas_call x1, Pallas kernels, shards(): pl.pallas_call(step_kernel, out_shape=(shape((2, ROWS, COLS)), shape((2,...  121 us
    pallas_call x1, Pallas kernels, shards(): pl.pallas_call(output_kernel, out_shape=(shape((2, ROWS, COLS)), shape((2...  13.7 us

profile of v2, /device:TPU:1, one launch (start us, length us, event | category | flops | bytes accessed | tf_op | source)
XLA Modules:
  0.0 135.2 jit_solution(10292216413451136512)
XLA Ops:
  0.6 120.9 %step.1 = (bf16[2,256,3584]{2,1,0:T(8,128)(2,1)}, bf16[2,4,4,224,512]{4,3,2,1,0:T(8,128)(2,1)}, f32[2,8,512]{2,1,0:T(8,128)}, bf16[2,256,512]{2,1,0:T(8,128)(2,1)}) custom-call(bf16[1,2,256,3584]{3,2,1,0:T(8,128)(2,1)} %grads.1, bf16[2,256,3584]{2,1,0:T(8,128)(2,1)} %momentum.1, bf16[2,3584,512]{2,1,0:T(8,128)(2,1)} %basis.1), custom_call_target="tpu_custom_call" | custom-call | tf_op jit(solution)/shard_map/step/pallas_call | solution.py:554
  121.5 13.7 %outputs.1 = (bf16[2,256,3584]{2,1,0:T(8,128)(2,1)}, bf16[2,256,3584]{2,1,0:T(8,128)(2,1)}, bf16[2,3584,512]{2,1,0:T(8,128)(2,1)}) custom-call(bf16[2,256,512]{2,1,0:T(8,128)(2,1)} %get-tuple-element.7.left, bf16[2,3584,512]{2,1,0:T(8,128)(2,1)} %bitcast.1, bf16[2,256,3584]{2,1,0:T(8,128)(2,1)} %get-tuple-element.9.blended, f32[2,8,512]{2,1,0:T(8,128)} %get-tuple-element.10.norms), custom_call_target="tpu_custom_call" | custom-call | tf_op jit(solution)/shard_map/outputs/pallas_call | solution.py:604

commit v3 on v2

--- a/solution.py
+++ b/solution.py
@@ -23,6 +23,7 @@
 STEP = 512
 PANEL = 16
 BLOCK = 128
+CHUNKS = 4
 
 momentum_decay = 0.95
 
@@ -79,7 +80,7 @@
     return pl.ds(start + half * (size // 2), size // 2)
 
 
-def projected_rings(full, y, x, z, send, recv):
+def projected_gather(full, y, x, z, send, recv):
     parts = ((0, 32, 0, 384), (32, 32, 0, 384), (0, 64, 384, 128))
 
     def cut(part, half):
@@ -88,41 +89,32 @@
 
     every = slice(None)
     plans = (
-        (0, 0, "tensor", lambda i: (y, x, i)),
-        (0, 1, "fsdp_0", lambda i: (i, x, every)),
-        (0, 2, "fsdp_1", lambda i: (every, i, every)),
-        (1, 0, "fsdp_1", lambda i: (y, i, z)),
-        (1, 1, "tensor", lambda i: (y, every, i)),
-        (1, 2, "fsdp_0", lambda i: (i, every, every)),
-        (2, 0, "fsdp_0", lambda i: (i, x, z)),
-        (2, 1, "fsdp_1", lambda i: (every, i, z)),
-        (2, 2, "tensor", lambda i: (every, every, i)),
+        ("tensor", "fsdp_0", "fsdp_1", lambda i: (y, x, i), lambda o, q: (shifted(y, o), shifted(x, q), every)),
+        ("fsdp_1", "tensor", "fsdp_0", lambda i: (y, i, z), lambda o, q: (shifted(y, q), every, shifted(z, o))),
+        ("fsdp_0", "fsdp_1", "tensor", lambda i: (i, x, z), lambda o, q: (every, shifted(x, o), shifted(z, q))),
     )
-    phases = ([], [], [])
-    for part, phase, axis, where in plans:
-        def at(i, half, part=part, where=where):
+    rings, spreads = [], []
+    for part, (first, line, side, ring_at, spread_at) in enumerate(plans):
+        def at_ring(i, half, part=part, where=ring_at):
             return full.at[(*where(i), *cut(part, half))]
 
-        phases[phase].append(Ring(axis, at, send.at[part, phase], recv.at[part, phase]))
-    return phases
+        def at_spread(o, q, half, part=part, where=spread_at):
+            return full.at[(*where(o, q), *cut(part, half))]
+
+        rings.append(Ring(first, at_ring, send.at[part, 0], recv.at[part, 0]))
+        spreads.append(Spread(at_spread, line, side, send.at[part, 1], recv.at[part, 1]))
+    return rings, spreads
 
 
 class Spread:
-    def __init__(self, part, r, y, x, held, out, send, recv, store):
-        self.part, self.r, self.held, self.out, self.store = part, r, held, out, store
-        self.send, self.recv = send.at[part], recv.at[part]
-        self.line_axis, self.side_axis = ("fsdp_0", "fsdp_1") if part == 0 else ("fsdp_1", "fsdp_0")
-        self.a, self.b = (y, x) if part == 0 else (x, y)
+    def __init__(self, at, line_axis, side_axis, send, recv, hand=None):
+        self.at, self.send, self.recv = at, send, recv
+        self.line_axis, self.side_axis = line_axis, side_axis
+        self.hand = hand or (lambda o, q: None)
         self.sent = []
-        self.stored = []
-
-    def ref(self, o, q, half=None):
-        i, j = shifted(self.a, o), shifted(self.b, q)
-        place = (i, j) if self.part == 0 else (j, i)
-        return (*place, rows_of(0, PIECE, half), pl.ds(self.part * (RANK // 2), RANK // 2))
 
     def copy(self, k, o, q, axis, way, half=None):
-        ref = self.held.at[self.ref(o, q, half)]
+        ref = self.at(o, q, half)
         return pltpu.make_async_remote_copy(
             src_ref=ref,
             dst_ref=ref,
@@ -137,30 +129,11 @@
         copy.start()
         self.sent.append(copy)
 
-    def hand_over(self, o, q):
-        k = 16 + 4 * o + q
-        ref = self.ref(o, q)
-        copy = pltpu.make_async_remote_copy(
-            src_ref=self.held.at[ref],
-            dst_ref=self.out.at[(self.r, *ref)],
-            send_sem=self.send.at[k],
-            recv_sem=self.recv.at[k],
-            device_id={"replica": 1 - self.r},
-            device_id_type=MESH,
-        )
-        copy.start()
-        self.sent.append(copy)
-        kept = pltpu.make_async_copy(
-            self.held.at[ref], self.out.at[(self.r, *ref)], self.store.at[3 + 16 * self.part + 4 * o + q]
-        )
-        kept.start()
-        self.stored.append(kept)
-
     def begin(self):
         self.go(0, 0, 0, self.line_axis, 1)
         self.go(1, 0, 0, self.line_axis, 3)
         self.sides(0)
-        self.hand_over(0, 0)
+        self.hand(0, 0)
 
     def sides(self, o):
         self.go(4 + o, o, 0, self.side_axis, 1)
@@ -177,10 +150,10 @@
             self.copy(2, 2, 0, self.line_axis, 1, 0).wait_recv()
             self.copy(3, 2, 0, self.line_axis, 3, 1).wait_recv()
         self.sides(o)
-        self.hand_over(o, 0)
+        self.hand(o, 0)
 
     def side(self, o):
-        first, second = ((3, 1) if o in (0, 3) else (1, 3))
+        first, second = (3, 1) if o in (0, 3) else (1, 3)
         for q in (first, second):
             if q == 3:
                 self.copy(4 + o, o, 3, self.side_axis, 1).wait_recv()
@@ -188,29 +161,23 @@
                 self.copy(8 + o, o, 1, self.side_axis, 3).wait_recv()
             if q == first:
                 self.go(12 + o, o, q, self.side_axis, 4 - q)
-            self.hand_over(o, q)
+            self.hand(o, q)
 
     def last(self, o):
         self.copy(12 + o, o, 2, self.side_axis, 1 if o in (0, 3) else 3).wait_recv()
-        self.hand_over(o, 2)
+        self.hand(o, 2)
 
     def drain(self):
         for copy in self.sent:
             copy.wait_send()
-        for copy in self.stored:
-            copy.wait()
-        for o in range(4):
-            for q in range(4):
-                k = 16 + 4 * o + q
-                ref = self.out.at[(1 - self.r, *self.ref(o, q))]
-                pltpu.make_async_remote_copy(
-                    src_ref=ref,
-                    dst_ref=ref,
-                    send_sem=self.send.at[k],
-                    recv_sem=self.recv.at[k],
-                    device_id={"replica": 1 - self.r},
-                    device_id_type=MESH,
-                ).wait_recv()
+
+
+SPREAD_STEPS = (("line", 3), ("line", 1), ("side", 0), ("line", 2), ("side", 3), ("side", 1), ("side", 2))
+
+
+def together(spreads, job, *args):
+    for spread in spreads:
+        getattr(spread, job)(*args)
 
 
 def halves(value):
@@ -295,8 +262,8 @@
 
 def step_kernel(
     grads, momentum, basis, blended, gathered, norms, left,
-    m_v, g_v, gp_v, b_v, acc, flipped, out_z, in_z, full, turned, gram, low, work, inverse, total, own, rows_v, sums,
-    load, gs, gr, zs, zr, ags, agr, ts, tr, bs, br, s_n, r_n, s_p, r_p, store,
+    m_v, g_v, gp_v, b_v, acc, flipped, out_z, in_z, full, turned, gram, low, work, inverse, total, sums,
+    load, gs, gr, zs, zr, ags, agr, ts, tr, bs, br, s_n, r_n, s_p, r_p,
 ):
     r, y, x, z = coords()
     other = 1 - r
@@ -333,7 +300,7 @@
         grad_copy(c, cols).wait()
         both = g_v[:, cols].astype(F32) + gp_v[:, cols].astype(F32)
         value = (m_v[:, cols].astype(F32) + both).astype(BF16)
-        m_v[:, cols] = value
+        blended[r, :, cols] = value
         acc[...] += jnp.dot(value, b_v[cols, :], preferred_element_type=F32)
         return carry
 
@@ -356,7 +323,7 @@
 
     def flip(c, carry):
         cols = pl.ds(pl.multiple_of(c * STEP, STEP), STEP)
-        flipped[cols, :] = m_v[:, cols].T
+        flipped[cols, :] = blended[r, :, cols].T
         return carry
 
     lax.fori_loop(0, steps, flip, 0)
@@ -366,15 +333,13 @@
         piece = piece + in_z[k - 1].astype(F32)
     full[y, x, z] = piece.astype(BF16)
 
-    phases = projected_rings(full, y, x, z, ags, agr)
-    for phase in phases:
-        for ring in phase:
-            ring.start()
-        for ring in phase:
-            ring.middle()
-        if phase is not phases[-1]:
-            for ring in phase:
-                ring.end()
+    rings, wide = projected_gather(full, y, x, z, ags, agr)
+    together(rings, "start")
+    together(rings, "middle")
+    together(rings, "end")
+    together(wide, "begin")
+    for job, o in SPREAD_STEPS:
+        together(wide, job, o)
 
     def turn_copy(k):
         ty, tx = shifted(y, k // 4), shifted(x, k % 4)
@@ -412,48 +377,41 @@
             device_id_type=MESH,
         )
 
-    share = to_partner(m_v, blended.at[r], bs.at[0], br.at[0])
+    share = to_partner(blended.at[r], blended.at[r], bs.at[0], br.at[0])
     share.start()
-    keep = pltpu.make_async_copy(m_v, blended.at[r], store.at[0])
-    keep.start()
     turned[y, x] = flipped[pl.ds(pl.multiple_of((y * 4 + x) * PIECE, PIECE), PIECE), :]
-    for ring in phases[-1]:
-        ring.end()
+    for o in (0, 3, 1, 2):
+        together(wide, "last", o)
 
     gram[...] = jnp.zeros_like(gram)
 
     def add_gram(b, carry):
-        rows = full[b // 4, lax.rem(b, 4)].reshape(ROWS, RANK)
+        rows = full[b].reshape(4 * ROWS, RANK)
         gram[...] += lax.dot_general(rows, rows, (((0,), (0,)), ((), ())), preferred_element_type=F32)
         return carry
 
-    lax.fori_loop(0, 16, add_gram, 0)
+    lax.fori_loop(0, 4, add_gram, 0)
     factor_inverse(gram, low, work, inverse)
     high = low[...].astype(BF16)
     total[...] = jnp.zeros_like(total)
     dims = (((1,), (1,)), ((), ()))
 
-    def left_rows(by, bx):
-        rows = full[by, bx].reshape(ROWS, RANK)
+    def left_rows(rows):
         return lax.dot_general(rows, high, dims, preferred_element_type=F32).astype(BF16)
 
-    own[...] = left_rows(y, x)
-    keep_left = pltpu.make_async_copy(own, left.at[r], store.at[1])
-    keep_left.start()
-    share_left = to_partner(own, left.at[r], bs.at[1], br.at[1])
-    share_left.start()
     for k in range(1, 16):
         turn_copy(k).wait_send()
         turn_arrival(k).wait_recv()
 
     def add_back(b, carry):
-        by, bx = b // 4, lax.rem(b, 4)
-        total[...] += jnp.dot(turned[by, bx], left_rows(by, bx), preferred_element_type=F32)
+        rows = left_rows(full[b].reshape(4 * ROWS, RANK))
+        for bx in range(4):
+            total[...] += jnp.dot(turned[b, bx], rows[bx * ROWS : (bx + 1) * ROWS], preferred_element_type=F32)
         return carry
 
-    lax.fori_loop(0, 16, add_back, 0)
+    lax.fori_loop(0, 4, add_back, 0)
     value = total[...]
-    rows_v[y, x] = value.astype(BF16)
+    gathered[r, y, x] = value.astype(BF16)
 
     def sum_copy(phase, axis, k, me):
         return pltpu.make_async_remote_copy(
@@ -486,58 +444,99 @@
             sum_arrival(phase, axis, k, me).wait_recv()
         return (sums[phase, 0] + sums[phase, 1]) + (sums[phase, 2] + sums[phase, 3])
 
-    spreads = (Spread(0, r, y, x, rows_v, gathered, s_p, r_p, store), Spread(1, r, y, x, rows_v, gathered, s_p, r_p, store))
-
-    def both(job, *args):
-        for spread in spreads:
-            getattr(spread, job)(*args)
-
-    both("begin")
+    def spread_of(part):
+        cols = pl.ds(part * (RANK // 2), RANK // 2)
+        axes = ("fsdp_0", "fsdp_1") if part == 0 else ("fsdp_1", "fsdp_0")
+
+        def place(o, q):
+            return (shifted(y, o), shifted(x, q)) if part == 0 else (shifted(y, q), shifted(x, o))
+
+        def at(o, q, half):
+            return gathered.at[(r, *place(o, q), rows_of(0, PIECE, half), cols)]
+
+        def passing(weight, o, q):
+            ref = gathered.at[(weight, *place(o, q), slice(None), cols)]
+            k = 16 + 4 * o + q
+            return to_partner(ref, ref, s_p.at[part, k], r_p.at[part, k])
+
+        def hand(o, q):
+            passing(r, o, q).start()
+
+        return Spread(at, *axes, s_p.at[part], r_p.at[part], hand), passing
+
+    spreads, passings = zip(*(spread_of(part) for part in (0, 1)))
+    together(spreads, "begin")
     send_sums(0, "tensor", z, jnp.sum((value * value).reshape(PIECE // 8, 8, RANK), axis=0))
-    both("line", 3)
-    both("line", 1)
-    part_sums = take_sums(0, "tensor", z)
-    send_sums(1, "fsdp_1", x, part_sums)
-    both("side", 0)
-    both("line", 2)
-    both("side", 3)
-    part_sums = take_sums(1, "fsdp_1", x)
-    send_sums(2, "fsdp_0", y, part_sums)
-    both("side", 1)
-    part_sums = take_sums(2, "fsdp_0", y)
-    sums[3, 0] = part_sums
-    keep_norms = pltpu.make_async_copy(sums.at[3, 0], norms.at[r], store.at[2])
-    keep_norms.start()
-    share_norms = to_partner(sums.at[3, 0], norms.at[r], bs.at[2], br.at[2])
-    share_norms.start()
-    both("side", 2)
-    for sub in (0, 3, 1, 2):
-        both("last", sub)
-    both("drain")
-    for ring in phases[0] + phases[1] + phases[2]:
-        ring.drain()
+    left[r] = left_rows(full[y, x].reshape(ROWS, RANK))
+    share_left = to_partner(left.at[r], left.at[r], bs.at[1], br.at[1])
+    share_left.start()
+    for at_step, (job, o) in enumerate(SPREAD_STEPS):
+        together(spreads, job, o)
+        if at_step == 1:
+            send_sums(1, "fsdp_1", x, take_sums(0, "tensor", z))
+        elif at_step == 3:
+            send_sums(2, "fsdp_0", y, take_sums(1, "fsdp_1", x))
+        elif at_step == 5:
+            norms[r] = take_sums(2, "fsdp_0", y)
+            to_partner(norms.at[r], norms.at[r], bs.at[2], br.at[2]).start()
+    for o in (0, 3, 1, 2):
+        together(spreads, "last", o)
+    together(spreads, "drain")
+    together(rings, "drain")
+    together(wide, "drain")
     for phase, axis, me in ((0, "tensor", z), (1, "fsdp_1", x), (2, "fsdp_0", y)):
         for k in (1, 2, 3):
             sum_copy(phase, axis, k, me).wait_send()
-    for copy in (keep, keep_left, keep_norms):
-        copy.wait()
-    for copy in (share, share_left, share_norms):
-        copy.wait_send()
     for k, out in enumerate((blended, left, norms)):
+        to_partner(out.at[r], out.at[r], bs.at[k], br.at[k]).wait_send()
         to_partner(out.at[other], out.at[other], bs.at[k], br.at[k]).wait_recv()
-
-
-def output_kernel(left, back, blended, norms, momentum_new, update, basis_new):
-    squares = jnp.sum(norms[0], axis=0, keepdims=True)
-    inverse = 1.0 / (jnp.sqrt(squares) + 1e-06)
-    rows = back[0]
-    normed = (rows.astype(F32) * inverse).astype(BF16)
-    basis_new[0] = normed
+    for passing in passings:
+        for o in range(4):
+            for q in range(4):
+                passing(r, o, q).wait_send()
+                passing(other, o, q).wait_recv()
+
+
+def output_kernel(left, back, blended, norms, momentum_new, update, basis_new, mom_v, up_v, base_v, sems):
+    wide = COLS // CHUNKS
     dims = (((1,), (1,)), ((), ()))
-    feedback = lax.dot_general(left[0], rows, dims, preferred_element_type=F32)
-    momentum_new[0] = (blended[0].astype(F32) - (1.0 - momentum_decay) * feedback).astype(BF16)
     scale = math.sqrt(FEATURES * UNITS / RANK)
-    update[0] = (scale * lax.dot_general(left[0], normed, dims, preferred_element_type=F32)).astype(BF16)
+
+    def copies(i):
+        w, start = i // CHUNKS, pl.multiple_of(lax.rem(i, CHUNKS) * wide, wide)
+        part = pl.ds(start, wide)
+        return (
+            pltpu.make_async_copy(base_v.at[w, part, :], basis_new.at[w, part, :], sems.at[0, i]),
+            pltpu.make_async_copy(mom_v.at[w, :, part], momentum_new.at[w, :, part], sems.at[1, i]),
+            pltpu.make_async_copy(up_v.at[w, :, part], update.at[w, :, part], sems.at[2, i]),
+        )
+
+    def chunk(i, carry):
+        w, start = i // CHUNKS, pl.multiple_of(lax.rem(i, CHUNKS) * wide, wide)
+        part = pl.ds(start, wide)
+        base, mom, up = copies(i)
+        inverse = 1.0 / (jnp.sqrt(jnp.sum(norms[w], axis=0, keepdims=True)) + 1e-06)
+        rows, basis = back[w, part, :], left[w]
+        normed = (rows.astype(F32) * inverse).astype(BF16)
+        base_v[w, part, :] = normed
+        base.start()
+        feedback = lax.dot_general(basis, rows, dims, preferred_element_type=F32)
+        value = blended[w, :, part].astype(F32) - (1.0 - momentum_decay) * feedback
+        mom_v[w, :, part] = value.astype(BF16)
+        mom.start()
+        value = scale * lax.dot_general(basis, normed, dims, preferred_element_type=F32)
+        up_v[w, :, part] = value.astype(BF16)
+        up.start()
+        return carry
+
+    lax.fori_loop(0, 2 * CHUNKS, chunk, 0)
+
+    def finish(i, carry):
+        for copy in copies(i):
+            copy.wait()
+        return carry
+
+    lax.fori_loop(0, 2 * CHUNKS, finish, 0)
 
 
 def shape(dims, dtype=BF16):
@@ -545,7 +544,7 @@
 
 
 VM = pl.BlockSpec(memory_space=pltpu.VMEM)
-ANY = pl.BlockSpec(memory_space=pl.ANY)
+HBM = pl.BlockSpec(memory_space=pltpu.HBM)
 DMA = pltpu.SemaphoreType.DMA
 
 
@@ -559,8 +558,8 @@
             shape((2, 8, RANK), F32),
             shape((2, ROWS, RANK)),
         ),
-        in_specs=[ANY] * 3,
-        out_specs=(ANY,) * 4,
+        in_specs=[HBM] * 3,
+        out_specs=(VM,) * 4,
         scratch_shapes=[
             pltpu.VMEM((ROWS, COLS), BF16),
             pltpu.VMEM((ROWS, COLS), BF16),
@@ -577,16 +576,14 @@
             pltpu.VMEM((BLOCK, 2 * BLOCK), F32),
             pltpu.VMEM((BLOCK, BLOCK), F32),
             pltpu.VMEM((PIECE, RANK), F32),
-            pltpu.VMEM((ROWS, RANK), BF16),
-            pltpu.VMEM((4, 4, PIECE, RANK), BF16),
-            pltpu.VMEM((4, 4, 8, RANK), F32),
+            pltpu.VMEM((3, 4, 8, RANK), F32),
             DMA((3, steps)),
             DMA((steps,)),
             DMA((steps,)),
             DMA((3,)),
             DMA((3,)),
-            DMA((3, 3, 4)),
-            DMA((3, 3, 4)),
+            DMA((3, 2, 16)),
+            DMA((3, 2, 16)),
             DMA((16,)),
             DMA((16,)),
             DMA((3,)),
@@ -595,27 +592,22 @@
             DMA((3, 3)),
             DMA((2, 32)),
             DMA((2, 32)),
-            DMA((35,)),
         ],
-        compiler_params=pltpu.CompilerParams(has_side_effects=True),
+        compiler_params=pltpu.CompilerParams(has_side_effects=True, vmem_limit_bytes=51 << 20),
         name="step",
     )(grads, momentum, basis)
-    wide = COLS // 4
     return pl.pallas_call(
         output_kernel,
         out_shape=(shape((2, ROWS, COLS)), shape((2, ROWS, COLS)), shape((2, COLS, RANK))),
-        grid=(2, 4),
-        in_specs=[
-            pl.BlockSpec((1, ROWS, RANK), lambda w, c: (w, 0, 0)),
-            pl.BlockSpec((1, wide, RANK), lambda w, c: (w, c, 0)),
-            pl.BlockSpec((1, ROWS, wide), lambda w, c: (w, 0, c)),
-            pl.BlockSpec((1, 8, RANK), lambda w, c: (w, 0, 0)),
+        in_specs=[VM] * 4,
+        out_specs=(HBM,) * 3,
+        scratch_shapes=[
+            pltpu.VMEM((2, ROWS, COLS), BF16),
+            pltpu.VMEM((2, ROWS, COLS), BF16),
+            pltpu.VMEM((2, COLS, RANK), BF16),
+            DMA((3, 2 * CHUNKS)),
         ],
-        out_specs=(
-            pl.BlockSpec((1, ROWS, wide), lambda w, c: (w, 0, c)),
-            pl.BlockSpec((1, ROWS, wide), lambda w, c: (w, 0, c)),
-            pl.BlockSpec((1, wide, RANK), lambda w, c: (w, c, 0)),
-        ),
+        compiler_params=pltpu.CompilerParams(vmem_limit_bytes=24 << 20),
         name="outputs",
     )(left, gathered.reshape(2, COLS, RANK), blended, norms)
 

time: 136 us -> 125 us (0.919)
  Pallas kernels: 135 us -> 119 us
  local copies, waits for them, and re-layouts: 0 us -> 5.11 us
    pallas_call x1, Pallas kernels: 121 us -> 111 us  [shards(): pl.pallas_call(step_kernel, out_shape=(shape((2, ROWS, COLS)), shape((2,...]
    pallas_call x1, Pallas kernels: 13.7 us -> 7.67 us  [shards(): pl.pallas_call(output_kernel, out_shape=(shape((2, ROWS, COLS)), shape((2...]
    unnamed x0 -> x4, local copies, waits for them, and re-layouts: none -> 5.11 us
where the time goes in v3:
time: 125 us
  Pallas kernels  119 us (95%)
  local copies, waits for them, and re-layouts  5.11 us (4%)
    pallas_call x1, Pallas kernels, shards(): pl.pallas_call(step_kernel, out_shape=(shape((2, ROWS, COLS)), shape((2,...  111 us
    pallas_call x1, Pallas kernels, shards(): pl.pallas_call(output_kernel, out_shape=(shape((2, ROWS, COLS)), shape((2...  7.67 us
    unnamed x4, local copies, waits for them, and re-layouts  5.11 us

profile of v3, /device:TPU:1, one launch (start us, length us, event | category | flops | bytes accessed | tf_op | source)
XLA Modules:
  0.0 124.7 jit_solution(12983610936026908731)
XLA Ops:
  0.6 111.2 %step.1 = (bf16[2,256,3584]{2,1,0:T(8,128)(2,1)}, bf16[2,4,4,224,512]{4,3,2,1,0:T(8,128)(2,1)}, f32[2,8,512]{2,1,0:T(8,128)S(1)}, bf16[2,256,512]{2,1,0:T(8,128)(2,1)S(1)}) custom-call(bf16[1,2,256,3584]{3,2,1,0:T(8,128)(2,1)} %grads.1, bf16[2,256,3584]{2,1,0:T(8,128)(2,1)} %momentum.1, bf16[2,3584,512]{2,1,0:T(8,128)(2,1)} %basis.1), custom_call_target="tpu_custom_call" | custom-call | tf_op jit(solution)/shard_map/step/pallas_call | solution.py:553
  111.9 0.0 copy-start
  111.9 3.1 %copy-done = bf16[2,4,4,224,512]{4,3,2,1,0:T(8,128)(2,1)S(1)} copy-done((bf16[2,4,4,224,512]{4,3,2,1,0:T(8,128)(2,1)S(1)}, bf16[2,4,4,224,512]{4,3,2,1,0:T(8,128)(2,1)}, u32[]{:S(2)}) %copy-start) | copy-done | bytes 7340056
  115.0 0.0 copy-start.1
  115.0 2.0 %copy-done.1 = bf16[2,256,3584]{2,1,0:T(8,128)(2,1)S(1)} copy-done((bf16[2,256,3584]{2,1,0:T(8,128)(2,1)S(1)}, bf16[2,256,3584]{2,1,0:T(8,128)(2,1)}, u32[]{:S(2)}) %copy-start.1) | copy-done | bytes 3670040
  117.0 7.7 %outputs.1 = (bf16[2,256,3584]{2,1,0:T(8,128)(2,1)}, bf16[2,256,3584]{2,1,0:T(8,128)(2,1)}, bf16[2,3584,512]{2,1,0:T(8,128)(2,1)}) custom-call(bf16[2,256,512]{2,1,0:T(8,128)(2,1)S(1)} %get-tuple-element.7.left, bf16[2,3584,512]{2,1,0:T(8,128)(2,1)S(1)} %bitcast.1, bf16[2,256,3584]{2,1,0:T(8,128)(2,1)S(1)} %copy-done.1, f32[2,8,512]{2,1,0:T(8,128)S(1)} %get-tuple-element.10.norms), custom_call_target="tpu_custom_call" | custom-call | tf_op jit(solution)/shard_map/outputs/pallas_call | solution.py:599
Async XLA Ops:
  111.9 3.1 %copy-start = (bf16[2,4,4,224,512]{4,3,2,1,0:T(8,128)(2,1)S(1)}, bf16[2,4,4,224,512]{4,3,2,1,0:T(8,128)(2,1)}, u32[]{:S(2)}) copy-start(bf16[2,4,4,224,512]{4,3,2,1,0:T(8,128)(2,1)} %get-tuple-element.8) | copy-start | bytes 22020100
  115.0 2.0 %copy-start.1 = (bf16[2,256,3584]{2,1,0:T(8,128)(2,1)S(1)}, bf16[2,256,3584]{2,1,0:T(8,128)(2,1)}, u32[]{:S(2)}) copy-start(bf16[2,256,3584]{2,1,0:T(8,128)(2,1)} %get-tuple-element.9.blended) | copy-start | bytes 11010052

commit v4 on v3

--- a/solution.py
+++ b/solution.py
@@ -260,8 +260,17 @@
             low[after, done] = low[after, done] - contract_rows(upper, low[here, done])
 
 
+def meet(y, x, z, other):
+    barrier = pltpu.get_barrier_semaphore()
+    peers = [{"replica": other}] + [{"tensor": shifted(z, k)} for k in (1, 2, 3)]
+    peers += [{"fsdp_0": shifted(y, k // 4), "fsdp_1": shifted(x, k % 4)} for k in range(1, 16)]
+    for peer in peers:
+        pl.semaphore_signal(barrier, inc=1, device_id=peer, device_id_type=MESH)
+    pl.semaphore_wait(barrier, len(peers))
+
+
 def step_kernel(
-    grads, momentum, basis, blended, gathered, norms, left,
+    grads, momentum, basis, blended, blended_too, gathered, gathered_too, norms, left,
     m_v, g_v, gp_v, b_v, acc, flipped, out_z, in_z, full, turned, gram, low, work, inverse, total, sums,
     load, gs, gr, zs, zr, ags, agr, ts, tr, bs, br, s_n, r_n, s_p, r_p,
 ):
@@ -287,10 +296,11 @@
         )
 
     for c in range(steps):
-        cols = pl.ds(c * STEP, STEP)
-        grad_copy(c, cols).start()
-        for copy in loads(c, cols):
+        for copy in loads(c, pl.ds(c * STEP, STEP)):
             copy.start()
+    meet(y, x, z, other)
+    for c in range(steps):
+        grad_copy(c, pl.ds(c * STEP, STEP)).start()
     acc[...] = jnp.zeros_like(acc)
 
     def blend(c, carry):
@@ -300,7 +310,7 @@
         grad_copy(c, cols).wait()
         both = g_v[:, cols].astype(F32) + gp_v[:, cols].astype(F32)
         value = (m_v[:, cols].astype(F32) + both).astype(BF16)
-        blended[r, :, cols] = value
+        blended[:, cols] = value
         acc[...] += jnp.dot(value, b_v[cols, :], preferred_element_type=F32)
         return carry
 
@@ -323,7 +333,7 @@
 
     def flip(c, carry):
         cols = pl.ds(pl.multiple_of(c * STEP, STEP), STEP)
-        flipped[cols, :] = blended[r, :, cols].T
+        flipped[cols, :] = blended[:, cols].T
         return carry
 
     lax.fori_loop(0, steps, flip, 0)
@@ -377,7 +387,7 @@
             device_id_type=MESH,
         )
 
-    share = to_partner(blended.at[r], blended.at[r], bs.at[0], br.at[0])
+    share = to_partner(blended, blended_too, bs.at[0], br.at[0])
     share.start()
     turned[y, x] = flipped[pl.ds(pl.multiple_of((y * 4 + x) * PIECE, PIECE), PIECE), :]
     for o in (0, 3, 1, 2):
@@ -411,7 +421,7 @@
 
     lax.fori_loop(0, 4, add_back, 0)
     value = total[...]
-    gathered[r, y, x] = value.astype(BF16)
+    gathered[y, x] = value.astype(BF16)
 
     def sum_copy(phase, axis, k, me):
         return pltpu.make_async_remote_copy(
@@ -452,23 +462,23 @@
             return (shifted(y, o), shifted(x, q)) if part == 0 else (shifted(y, q), shifted(x, o))
 
         def at(o, q, half):
-            return gathered.at[(r, *place(o, q), rows_of(0, PIECE, half), cols)]
-
-        def passing(weight, o, q):
-            ref = gathered.at[(weight, *place(o, q), slice(None), cols)]
+            return gathered.at[(*place(o, q), rows_of(0, PIECE, half), cols)]
+
+        def passing(o, q):
+            where = (*place(o, q), slice(None), cols)
             k = 16 + 4 * o + q
-            return to_partner(ref, ref, s_p.at[part, k], r_p.at[part, k])
+            return to_partner(gathered.at[where], gathered_too.at[where], s_p.at[part, k], r_p.at[part, k])
 
         def hand(o, q):
-            passing(r, o, q).start()
+            passing(o, q).start()
 
         return Spread(at, *axes, s_p.at[part], r_p.at[part], hand), passing
 
     spreads, passings = zip(*(spread_of(part) for part in (0, 1)))
     together(spreads, "begin")
     send_sums(0, "tensor", z, jnp.sum((value * value).reshape(PIECE // 8, 8, RANK), axis=0))
-    left[r] = left_rows(full[y, x].reshape(ROWS, RANK))
-    share_left = to_partner(left.at[r], left.at[r], bs.at[1], br.at[1])
+    left[0] = left_rows(full[y, x].reshape(ROWS, RANK))
+    share_left = to_partner(left.at[0], left.at[1], bs.at[1], br.at[1])
     share_left.start()
     for at_step, (job, o) in enumerate(SPREAD_STEPS):
         together(spreads, job, o)
@@ -477,8 +487,9 @@
         elif at_step == 3:
             send_sums(2, "fsdp_0", y, take_sums(1, "fsdp_1", x))
         elif at_step == 5:
-            norms[r] = take_sums(2, "fsdp_0", y)
-            to_partner(norms.at[r], norms.at[r], bs.at[2], br.at[2]).start()
+            norms[0] = take_sums(2, "fsdp_0", y)
+            share_norms = to_partner(norms.at[0], norms.at[1], bs.at[2], br.at[2])
+            share_norms.start()
     for o in (0, 3, 1, 2):
         together(spreads, "last", o)
     together(spreads, "drain")
@@ -487,56 +498,58 @@
     for phase, axis, me in ((0, "tensor", z), (1, "fsdp_1", x), (2, "fsdp_0", y)):
         for k in (1, 2, 3):
             sum_copy(phase, axis, k, me).wait_send()
-    for k, out in enumerate((blended, left, norms)):
-        to_partner(out.at[r], out.at[r], bs.at[k], br.at[k]).wait_send()
-        to_partner(out.at[other], out.at[other], bs.at[k], br.at[k]).wait_recv()
+    share.wait()
+    share_left.wait()
+    share_norms.wait()
     for passing in passings:
         for o in range(4):
             for q in range(4):
-                passing(r, o, q).wait_send()
-                passing(other, o, q).wait_recv()
-
-
-def output_kernel(left, back, blended, norms, momentum_new, update, basis_new, mom_v, up_v, base_v, sems):
+                passing(o, q).wait()
+
+
+def output_kernel(left, back, back_too, blended, blended_too, norms, momentum_new, update, basis_new, mom_v, up_v, base_v, sems):
     wide = COLS // CHUNKS
     dims = (((1,), (1,)), ((), ()))
     scale = math.sqrt(FEATURES * UNITS / RANK)
-
-    def copies(i):
-        w, start = i // CHUNKS, pl.multiple_of(lax.rem(i, CHUNKS) * wide, wide)
-        part = pl.ds(start, wide)
-        return (
-            pltpu.make_async_copy(base_v.at[w, part, :], basis_new.at[w, part, :], sems.at[0, i]),
-            pltpu.make_async_copy(mom_v.at[w, :, part], momentum_new.at[w, :, part], sems.at[1, i]),
-            pltpu.make_async_copy(up_v.at[w, :, part], update.at[w, :, part], sems.at[2, i]),
-        )
-
-    def chunk(i, carry):
-        w, start = i // CHUNKS, pl.multiple_of(lax.rem(i, CHUNKS) * wide, wide)
-        part = pl.ds(start, wide)
-        base, mom, up = copies(i)
-        inverse = 1.0 / (jnp.sqrt(jnp.sum(norms[w], axis=0, keepdims=True)) + 1e-06)
-        rows, basis = back[w, part, :], left[w]
-        normed = (rows.astype(F32) * inverse).astype(BF16)
-        base_v[w, part, :] = normed
-        base.start()
-        feedback = lax.dot_general(basis, rows, dims, preferred_element_type=F32)
-        value = blended[w, :, part].astype(F32) - (1.0 - momentum_decay) * feedback
-        mom_v[w, :, part] = value.astype(BF16)
-        mom.start()
-        value = scale * lax.dot_general(basis, normed, dims, preferred_element_type=F32)
-        up_v[w, :, part] = value.astype(BF16)
-        up.start()
-        return carry
-
-    lax.fori_loop(0, 2 * CHUNKS, chunk, 0)
-
-    def finish(i, carry):
-        for copy in copies(i):
-            copy.wait()
-        return carry
-
-    lax.fori_loop(0, 2 * CHUNKS, finish, 0)
+    me = lax.axis_index("replica")
+
+    def copies(half, i):
+        part = pl.ds(pl.multiple_of(i * wide, wide), wide)
+        w = me if half == 0 else 1 - me
+        return part, (
+            pltpu.make_async_copy(base_v.at[half, part, :], basis_new.at[w, part, :], sems.at[0, half, i]),
+            pltpu.make_async_copy(mom_v.at[half, :, part], momentum_new.at[w, :, part], sems.at[1, half, i]),
+            pltpu.make_async_copy(up_v.at[half, :, part], update.at[w, :, part], sems.at[2, half, i]),
+        )
+
+    for half, (rows_ref, old) in enumerate(((back, blended), (back_too, blended_too))):
+        inverse = 1.0 / (jnp.sqrt(jnp.sum(norms[half], axis=0, keepdims=True)) + 1e-06)
+        basis = left[half]
+
+        def chunk(i, carry, half=half, rows_ref=rows_ref, old=old, inverse=inverse, basis=basis):
+            part, (base, mom, up) = copies(half, i)
+            rows = rows_ref[part, :]
+            normed = (rows.astype(F32) * inverse).astype(BF16)
+            base_v[half, part, :] = normed
+            base.start()
+            feedback = lax.dot_general(basis, rows, dims, preferred_element_type=F32)
+            value = old[:, part].astype(F32) - (1.0 - momentum_decay) * feedback
+            mom_v[half, :, part] = value.astype(BF16)
+            mom.start()
+            value = scale * lax.dot_general(basis, normed, dims, preferred_element_type=F32)
+            up_v[half, :, part] = value.astype(BF16)
+            up.start()
+            return carry
+
+        lax.fori_loop(0, CHUNKS, chunk, 0)
+    for half in range(2):
+
+        def finish(i, carry, half=half):
+            for copy in copies(half, i)[1]:
+                copy.wait()
+            return carry
+
+        lax.fori_loop(0, CHUNKS, finish, 0)
 
 
 def shape(dims, dtype=BF16):
@@ -550,16 +563,18 @@
 
 def shards(grads, momentum, basis):
     steps = COLS // STEP
-    blended, gathered, norms, left = pl.pallas_call(
+    blended, blended_too, gathered, gathered_too, norms, left = pl.pallas_call(
         step_kernel,
         out_shape=(
-            shape((2, ROWS, COLS)),
-            shape((2, 4, 4, PIECE, RANK)),
+            shape((ROWS, COLS)),
+            shape((ROWS, COLS)),
+            shape((4, 4, PIECE, RANK)),
+            shape((4, 4, PIECE, RANK)),
             shape((2, 8, RANK), F32),
             shape((2, ROWS, RANK)),
         ),
         in_specs=[HBM] * 3,
-        out_specs=(VM,) * 4,
+        out_specs=(VM,) * 6,
         scratch_shapes=[
             pltpu.VMEM((ROWS, COLS), BF16),
             pltpu.VMEM((ROWS, COLS), BF16),
@@ -593,23 +608,23 @@
             DMA((2, 32)),
             DMA((2, 32)),
         ],
-        compiler_params=pltpu.CompilerParams(has_side_effects=True, vmem_limit_bytes=51 << 20),
+        compiler_params=pltpu.CompilerParams(collective_id=0, has_side_effects=True, vmem_limit_bytes=42 << 20),
         name="step",
     )(grads, momentum, basis)
     return pl.pallas_call(
         output_kernel,
         out_shape=(shape((2, ROWS, COLS)), shape((2, ROWS, COLS)), shape((2, COLS, RANK))),
-        in_specs=[VM] * 4,
+        in_specs=[VM] * 6,
         out_specs=(HBM,) * 3,
         scratch_shapes=[
             pltpu.VMEM((2, ROWS, COLS), BF16),
             pltpu.VMEM((2, ROWS, COLS), BF16),
             pltpu.VMEM((2, COLS, RANK), BF16),
-            DMA((3, 2 * CHUNKS)),
+            DMA((3, 2, CHUNKS)),
         ],
         compiler_params=pltpu.CompilerParams(vmem_limit_bytes=24 << 20),
         name="outputs",
-    )(left, gathered.reshape(2, COLS, RANK), blended, norms)
+    )(left, gathered.reshape(COLS, RANK), gathered_too.reshape(COLS, RANK), blended, blended_too, norms)
 
 
 def solution(mesh):

time: 125 us -> 110 us (0.88)
  Pallas kernels: 119 us -> 110 us
  local copies, waits for them, and re-layouts: 5.11 us -> 0 us
    pallas_call x1, Pallas kernels: 111 us -> 102 us  [shards(): pl.pallas_call(step_kernel, out_shape=(shape((ROWS, COLS)), shape((ROWS,...]
    unnamed x4 -> x0, local copies, waits for them, and re-layouts: 5.11 us -> none
where the time goes in v4:
time: 110 us
  Pallas kernels  110 us (100%)
    pallas_call x1, Pallas kernels, shards(): pl.pallas_call(step_kernel, out_shape=(shape((ROWS, COLS)), shape((ROWS,...  102 us
    pallas_call x1, Pallas kernels, shards(): pl.pallas_call(output_kernel, out_shape=(shape((2, ROWS, COLS)), shape((2...  7.71 us

profile of v4, /device:TPU:1, one launch (start us, length us, event | category | flops | bytes accessed | tf_op | source)
XLA Modules:
  0.0 110.3 jit_solution(16079670169810293160)
XLA Ops:
  0.6 101.9 %step.1 = (bf16[256,3584]{1,0:T(8,128)(2,1)S(1)}, bf16[256,3584]{1,0:T(8,128)(2,1)S(1)}, bf16[4,4,224,512]{3,2,1,0:T(8,128)(2,1)S(1)}, bf16[4,4,224,512]{3,2,1,0...) custom-call(bf16[1,2,256,3584]{3,2,1,0:T(8,128)(2,1)} %grads.1, ...), custom_call_target="tpu_custom_call" | custom-call | tf_op jit(solution)/shard_map/step/pallas_call | solution.py:566
  102.6 7.7 %outputs.1 = (bf16[2,256,3584]{2,1,0:T(8,128)(2,1)}, bf16[2,256,3584]{2,1,0:T(8,128)(2,1)}, bf16[2,3584,512]{2,1,0:T(8,128)(2,1)}) custom-call(bf16[2,256,512]{2,1,0:T(8,128)(2,1)S(1)} %get-tuple-element.9.left, bf16[3584,512]{1,0:T(8,128)(2,1)S(1)} %bitcast.2, bf16[3584,512]{1,0:T(8,128)(2,1)S(1)} %bitcast.3, ...), custom_call_target="tpu_custom_call" | custom-call | tf_op jit(solution)/shard_map/outputs/pallas_call | solution.py:614

commit v5 on v4

--- a/solution.py
+++ b/solution.py
@@ -39,39 +39,30 @@
 class Ring:
     def __init__(self, axis, at, send, recv):
         self.axis, self.at, self.send, self.recv = axis, at, send, recv
-        me = lax.axis_index(axis)
-        self.me, self.right, self.left, self.far = me, shifted(me, 1), shifted(me, 3), shifted(me, 2)
-
-    def copy(self, k, who, half, to):
-        ref = self.at(who, half)
+
+    def copy(self, k, arriving):
+        me = lax.axis_index(self.axis)
+        ref = self.at(shifted(me, 4 - k) if arriving else me)
         return pltpu.make_async_remote_copy(
             src_ref=ref,
             dst_ref=ref,
             send_sem=self.send.at[k],
             recv_sem=self.recv.at[k],
-            device_id={self.axis: to},
+            device_id={self.axis: shifted(me, k)},
             device_id_type=MESH,
         )
 
     def start(self):
-        self.copy(0, self.me, None, self.right).start()
-        self.copy(1, self.me, None, self.left).start()
-
-    def middle(self):
-        self.copy(0, self.left, None, self.right).wait_recv()
-        self.copy(2, self.left, 0, self.right).start()
-        self.copy(1, self.right, None, self.left).wait_recv()
-        self.copy(3, self.right, 1, self.left).start()
+        for k in (2, 1, 3):
+            self.copy(k, False).start()
 
     def end(self):
-        self.copy(2, self.far, 0, self.right).wait_recv()
-        self.copy(3, self.far, 1, self.left).wait_recv()
+        for k in (1, 3, 2):
+            self.copy(k, True).wait_recv()
 
     def drain(self):
-        self.copy(0, self.me, None, self.right).wait_send()
-        self.copy(1, self.me, None, self.left).wait_send()
-        self.copy(2, self.left, 0, self.right).wait_send()
-        self.copy(3, self.right, 1, self.left).wait_send()
+        for k in (1, 2, 3):
+            self.copy(k, False).wait_send()
 
 
 def rows_of(start, size, half):
@@ -95,8 +86,8 @@
     )
     rings, spreads = [], []
     for part, (first, line, side, ring_at, spread_at) in enumerate(plans):
-        def at_ring(i, half, part=part, where=ring_at):
-            return full.at[(*where(i), *cut(part, half))]
+        def at_ring(i, part=part, where=ring_at):
+            return full.at[(*where(i), *cut(part, None))]
 
         def at_spread(o, q, half, part=part, where=spread_at):
             return full.at[(*where(o, q), *cut(part, half))]
@@ -202,6 +193,17 @@
     return jnp.dot(
         jnp.concatenate([ah, ah, al], axis=1),
         jnp.concatenate([bh, bl, bh], axis=0),
+        preferred_element_type=F32,
+    )
+
+
+def times_transpose(a, b):
+    ah, al = halves(a)
+    bh, bl = halves(b)
+    return lax.dot_general(
+        jnp.concatenate([ah, ah, al], axis=1),
+        jnp.concatenate([bh, bl, bh], axis=1),
+        (((1,), (1,)), ((), ())),
         preferred_element_type=F32,
     )
 
@@ -260,6 +262,9 @@
             low[after, done] = low[after, done] - contract_rows(upper, low[here, done])
 
 
+NEAR = (1, 3, 4, 12)
+
+
 def meet(y, x, z, other):
     barrier = pltpu.get_barrier_semaphore()
     peers = [{"replica": other}] + [{"tensor": shifted(z, k)} for k in (1, 2, 3)]
@@ -337,6 +342,20 @@
         return carry
 
     lax.fori_loop(0, steps, flip, 0)
+    def turn_copy(k):
+        ty, tx = shifted(y, k // 4), shifted(x, k % 4)
+        start = pl.multiple_of((ty * 4 + tx) * PIECE, PIECE)
+        return pltpu.make_async_remote_copy(
+            src_ref=flipped.at[pl.ds(start, PIECE), :],
+            dst_ref=turned.at[y, x],
+            send_sem=ts.at[k],
+            recv_sem=tr.at[k],
+            device_id={"fsdp_0": ty, "fsdp_1": tx},
+            device_id_type=MESH,
+        )
+
+    for k in NEAR:
+        turn_copy(k).start()
     piece = acc[pl.ds(pl.multiple_of(z * SLICE, SLICE), SLICE), :]
     for k in (1, 3, 2):
         z_copy(k).wait()
@@ -345,23 +364,10 @@
 
     rings, wide = projected_gather(full, y, x, z, ags, agr)
     together(rings, "start")
-    together(rings, "middle")
     together(rings, "end")
     together(wide, "begin")
     for job, o in SPREAD_STEPS:
         together(wide, job, o)
-
-    def turn_copy(k):
-        ty, tx = shifted(y, k // 4), shifted(x, k % 4)
-        start = pl.multiple_of((ty * 4 + tx) * PIECE, PIECE)
-        return pltpu.make_async_remote_copy(
-            src_ref=flipped.at[pl.ds(start, PIECE), :],
-            dst_ref=turned.at[y, x],
-            send_sem=ts.at[k],
-            recv_sem=tr.at[k],
-            device_id={"fsdp_0": ty, "fsdp_1": tx},
-            device_id_type=MESH,
-        )
 
     def turn_arrival(k):
         sy, sx = shifted(y, 4 - k // 4), shifted(x, 4 - k % 4)
@@ -375,7 +381,8 @@
         )
 
     for k in range(1, 16):
-        turn_copy(k).start()
+        if k not in NEAR:
+            turn_copy(k).start()
 
     def to_partner(src, dst, send, recv):
         return pltpu.make_async_remote_copy(
@@ -414,13 +421,13 @@
         turn_arrival(k).wait_recv()
 
     def add_back(b, carry):
-        rows = left_rows(full[b].reshape(4 * ROWS, RANK))
-        for bx in range(4):
-            total[...] += jnp.dot(turned[b, bx], rows[bx * ROWS : (bx + 1) * ROWS], preferred_element_type=F32)
+        rows = full[b].reshape(4 * ROWS, RANK)
+        columns = jnp.concatenate([turned[b, bx] for bx in range(4)], axis=1)
+        total[...] += jnp.dot(columns, rows, preferred_element_type=F32)
         return carry
 
     lax.fori_loop(0, 4, add_back, 0)
-    value = total[...]
+    value = times_transpose(total[...], low[...])
     gathered[y, x] = value.astype(BF16)
 
     def sum_copy(phase, axis, k, me):
@@ -524,7 +531,7 @@
 
     for half, (rows_ref, old) in enumerate(((back, blended), (back_too, blended_too))):
         inverse = 1.0 / (jnp.sqrt(jnp.sum(norms[half], axis=0, keepdims=True)) + 1e-06)
-        basis = left[half]
+        basis = jnp.concatenate([left[half], (left[half].astype(F32) * inverse).astype(BF16)], axis=0)
 
         def chunk(i, carry, half=half, rows_ref=rows_ref, old=old, inverse=inverse, basis=basis):
             part, (base, mom, up) = copies(half, i)
@@ -532,12 +539,11 @@
             normed = (rows.astype(F32) * inverse).astype(BF16)
             base_v[half, part, :] = normed
             base.start()
-            feedback = lax.dot_general(basis, rows, dims, preferred_element_type=F32)
-            value = old[:, part].astype(F32) - (1.0 - momentum_decay) * feedback
+            product = lax.dot_general(basis, rows, dims, preferred_element_type=F32)
+            value = old[:, part].astype(F32) - (1.0 - momentum_decay) * product[:ROWS]
             mom_v[half, :, part] = value.astype(BF16)
             mom.start()
-            value = scale * lax.dot_general(basis, normed, dims, preferred_element_type=F32)
-            up_v[half, :, part] = value.astype(BF16)
+            up_v[half, :, part] = (scale * product[ROWS:]).astype(BF16)
             up.start()
             return carry
 

time: 110 us -> 112 us (1.018)
    pallas_call x1, Pallas kernels: 102 us -> 104 us  [shards(): pl.pallas_call(step_kernel, out_shape=(shape((ROWS, COLS)), shape((ROWS,...]
where the time goes in v5:
time: 112 us
  Pallas kernels  111 us (99%)
    pallas_call x1, Pallas kernels, shards(): pl.pallas_call(step_kernel, out_shape=(shape((ROWS, COLS)), shape((ROWS,...  104 us
    pallas_call x1, Pallas kernels, shards(): pl.pallas_call(output_kernel, out_shape=(shape((2, ROWS, COLS)), shape((2...  7.45 us

profile of v5, /device:TPU:1, one launch (start us, length us, event | category | flops | bytes accessed | tf_op | source)
XLA Modules:
  0.0 111.9 jit_solution(11310154054477681787)
XLA Ops:
  0.6 103.8 %step.1 = (bf16[256,3584]{1,0:T(8,128)(2,1)S(1)}, bf16[256,3584]{1,0:T(8,128)(2,1)S(1)}, bf16[4,4,224,512]{3,2,1,0:T(8,128)(2,1)S(1)}, bf16[4,4,224,512]{3,2,1,0...) custom-call(bf16[1,2,256,3584]{3,2,1,0:T(8,128)(2,1)} %grads.1, ...), custom_call_target="tpu_custom_call" | custom-call | tf_op jit(solution)/shard_map/step/pallas_call | solution.py:572
  104.4 7.5 %outputs.1 = (bf16[2,256,3584]{2,1,0:T(8,128)(2,1)}, bf16[2,256,3584]{2,1,0:T(8,128)(2,1)}, bf16[2,3584,512]{2,1,0:T(8,128)(2,1)}) custom-call(bf16[2,256,512]{2,1,0:T(8,128)(2,1)S(1)} %get-tuple-element.9.left, bf16[3584,512]{1,0:T(8,128)(2,1)S(1)} %bitcast.2, bf16[3584,512]{1,0:T(8,128)(2,1)S(1)} %bitcast.3, ...), custom_call_target="tpu_custom_call" | custom-call | tf_op jit(solution)/shard_map/outputs/pallas_call | solution.py:620

commit v6 on v5

--- a/solution.py
+++ b/solution.py
@@ -262,9 +262,6 @@
             low[after, done] = low[after, done] - contract_rows(upper, low[here, done])
 
 
-NEAR = (1, 3, 4, 12)
-
-
 def meet(y, x, z, other):
     barrier = pltpu.get_barrier_semaphore()
     peers = [{"replica": other}] + [{"tensor": shifted(z, k)} for k in (1, 2, 3)]
@@ -354,8 +351,6 @@
             device_id_type=MESH,
         )
 
-    for k in NEAR:
-        turn_copy(k).start()
     piece = acc[pl.ds(pl.multiple_of(z * SLICE, SLICE), SLICE), :]
     for k in (1, 3, 2):
         z_copy(k).wait()
@@ -381,8 +376,7 @@
         )
 
     for k in range(1, 16):
-        if k not in NEAR:
-            turn_copy(k).start()
+        turn_copy(k).start()
 
     def to_partner(src, dst, send, recv):
         return pltpu.make_async_remote_copy(

time: 112 us -> 105 us (0.938)
  Pallas kernels: 111 us -> 104 us
    pallas_call x1, Pallas kernels: 104 us -> 96.7 us  [shards(): pl.pallas_call(step_kernel, out_shape=(shape((ROWS, COLS)), shape((ROWS,...]
where the time goes in v6:
time: 105 us
  Pallas kernels  104 us (99%)
    pallas_call x1, Pallas kernels, shards(): pl.pallas_call(step_kernel, out_shape=(shape((ROWS, COLS)), shape((ROWS,...  96.7 us
    pallas_call x1, Pallas kernels, shards(): pl.pallas_call(output_kernel, out_shape=(shape((2, ROWS, COLS)), shape((2...  7.46 us

profile of v6, /device:TPU:1, one launch (start us, length us, event | category | flops | bytes accessed | tf_op | source)
XLA Modules:
  0.0 104.8 jit_solution(10467844274203291242)
XLA Ops:
  0.6 96.7 %step.1 = (bf16[256,3584]{1,0:T(8,128)(2,1)S(1)}, bf16[256,3584]{1,0:T(8,128)(2,1)S(1)}, bf16[4,4,224,512]{3,2,1,0:T(8,128)(2,1)S(1)}, bf16[4,4,224,512]{3,2,1,0...) custom-call(bf16[1,2,256,3584]{3,2,1,0:T(8,128)(2,1)} %grads.1, ...), custom_call_target="tpu_custom_call" | custom-call | tf_op jit(solution)/shard_map/step/pallas_call | solution.py:566
  97.3 7.5 %outputs.1 = (bf16[2,256,3584]{2,1,0:T(8,128)(2,1)}, bf16[2,256,3584]{2,1,0:T(8,128)(2,1)}, bf16[2,3584,512]{2,1,0:T(8,128)(2,1)}) custom-call(bf16[2,256,512]{2,1,0:T(8,128)(2,1)S(1)} %get-tuple-element.9.left, bf16[3584,512]{1,0:T(8,128)(2,1)S(1)} %bitcast.2, bf16[3584,512]{1,0:T(8,128)(2,1)S(1)} %bitcast.3, ...), custom_call_target="tpu_custom_call" | custom-call | tf_op jit(solution)/shard_map/outputs/pallas_call | solution.py:614

commit v7 on v6

--- a/solution.py
+++ b/solution.py
@@ -23,7 +23,7 @@
 STEP = 512
 PANEL = 16
 BLOCK = 128
-CHUNKS = 4
+CHUNKS = 2
 
 momentum_decay = 0.95
 

time: 105 us -> 104 us (level)
  no operation moved by 1% of the time
where the time goes in v7:
time: 104 us
  Pallas kernels  103 us (99%)
    pallas_call x1, Pallas kernels, shards(): pl.pallas_call(step_kernel, out_shape=(shape((ROWS, COLS)), shape((ROWS,...  96.7 us
    pallas_call x1, Pallas kernels, shards(): pl.pallas_call(output_kernel, out_shape=(shape((2, ROWS, COLS)), shape((2...  6.52 us

profile of v7, /device:TPU:1, one launch (start us, length us, event | category | flops | bytes accessed | tf_op | source)
XLA Modules:
  0.0 103.9 jit_solution(16759586335275537784)
XLA Ops:
  0.6 96.7 %step.1 = (bf16[256,3584]{1,0:T(8,128)(2,1)S(1)}, bf16[256,3584]{1,0:T(8,128)(2,1)S(1)}, bf16[4,4,224,512]{3,2,1,0:T(8,128)(2,1)S(1)}, bf16[4,4,224,512]{3,2,1,0...) custom-call(bf16[1,2,256,3584]{3,2,1,0:T(8,128)(2,1)} %grads.1, ...), custom_call_target="tpu_custom_call" | custom-call | tf_op jit(solution)/shard_map/step/pallas_call | solution.py:566
  97.3 6.5 %outputs.1 = (bf16[2,256,3584]{2,1,0:T(8,128)(2,1)}, bf16[2,256,3584]{2,1,0:T(8,128)(2,1)}, bf16[2,3584,512]{2,1,0:T(8,128)(2,1)}) custom-call(bf16[2,256,512]{2,1,0:T(8,128)(2,1)S(1)} %get-tuple-element.9.left, bf16[3584,512]{1,0:T(8,128)(2,1)S(1)} %bitcast.2, bf16[3584,512]{1,0:T(8,128)(2,1)S(1)} %bitcast.3, ...), custom_call_target="tpu_custom_call" | custom-call | tf_op jit(solution)/shard_map/outputs/pallas_call | solution.py:614
